TPU v7x, 256 devices: a whole 4x4x8 slice. The times are simulated.
256 devices in a mesh: dp: 32 (over x, z), tp: 8 (over y, core).
Axes of the slice: x: 4, y: 4, z: 8, core: 2. Of those that a mesh axis runs over, the one named last changes fastest.
Arguments:
- hidden_state: bfloat16 [7168, 512], P(None, 'dp'), may hold values from -6 to 6
- attention_gain: float32 [7168], replicated, may hold values from 0.1 to 1.9
- down_weight: bfloat16 [7168, 2112], P(None, 'tp'), may hold values from -0.0625 to 0.0625
- query_gain: float32 [1536], replicated, may hold values from 0.1 to 1.9
- latent_gain: float32 [512], replicated, may hold values from 0.1 to 1.9
- query_weight: bfloat16 [128, 576, 1536], P('tp', 'dp'), may hold values from -0.15625 to 0.15625
- latent_cache: bfloat16 [256, 4096, 576], P('dp'), may hold values from -240 to 240
- cache_length: int32 [256], P('dp'), may hold values from 1 to 4096
- owner_place: int32 [256], replicated, may hold values from 0 to 255, each once
- accept_length: int32 [256], replicated, may hold values from 1 to 2
- value_weight: bfloat16 [128, 512, 128], P('tp'), may hold values from -0.25 to 0.25
- output_weight: bfloat16 [7168, 16384], P('dp', 'tp'), may hold values from -0.046875 to 0.046875
- final_gain: float32 [7168], replicated, may hold values from 0.1 to 1.9
- head_weight: bfloat16 [7168, 65536], P(None, ('dp', 'tp')), may hold values from -8 to 8
- draft_tokens: int32 [256, 2], replicated, may hold values from 0 to 65535
Outputs:
- log_probs: float32 [512, 65536], P(None, ('dp', 'tp'))
- draft_scores: float32 [512], replicated
- committed: bfloat16 [256, 2, 576], P('dp')
All inputs are finite; a program needn't handle non-finite values.
Results may differ from a plain program's by a relative error of at most 0.006.
The roundings to bfloat16 on the way count: a program that leaves them out, or rounds other values in their place, can miss the bound.
Values may be sent and summed in bfloat16 or wider, within the bound.
No kernel may reach another device: no remote copies, remote signals or barrier semaphores. Data moves between devices by JAX's collectives and lax.ppermute only.
A program may use at most 192 MiB of HBM per device.

v0:
```python
import jax
import jax.numpy as jnp
from jax import lax
from jax.sharding import PartitionSpec as P

D = 7168
QL = 1536
DL = 512
DR = 64


epsilon = 1e-06
score_scale = 192.0 ** (-0.5)
masked_score = -1e30


def row_norm(values, gain_vector):
    inverse_rms = lax.rsqrt(jnp.mean(values * values, axis=-1, keepdims=True) + epsilon)
    return values * inverse_rms * gain_vector


def round_keep(values):
    return lax.optimization_barrier(values.astype(jnp.bfloat16)).astype(jnp.float32)


def on_device(
    hidden_state,
    attention_gain,
    down_weight,
    query_gain,
    latent_gain,
    query_weight,
    latent_cache,
    cache_length,
    owner_place,
    accept_length,
    value_weight,
    output_weight,
    final_gain,
    head_weight,
    draft_tokens,
):
    dp_count = lax.axis_size("dp")
    tp_count = lax.axis_size("tp")
    dp_rank = lax.axis_index("dp")
    tp_rank = lax.axis_index("tp")
    request_count = draft_tokens.shape[0]
    step_count = draft_tokens.shape[1]
    row_count = request_count * step_count
    local_requests = latent_cache.shape[0]
    local_rows = local_requests * step_count
    context = latent_cache.shape[1]
    slice_width = query_weight.shape[1]
    local_heads = value_weight.shape[0]
    value_width = value_weight.shape[2]
    stream = hidden_state.astype(jnp.float32)
    scaled = (stream * attention_gain[:, None]).astype(jnp.bfloat16)
    column_part = lax.dot_general(
        scaled, down_weight, (((0,), (0,)), ((), ())), preferred_element_type=jnp.float32
    )
    projected = lax.all_gather(column_part, "tp", axis=1, tiled=True)
    inverse_norm = lax.rsqrt(jnp.sum(stream * stream, axis=0) / D + epsilon)
    latent = projected * inverse_norm[:, None]
    query_latent = row_norm(latent[:, :QL], query_gain).astype(jnp.bfloat16)
    latent_part = row_norm(latent[:, QL : QL + DL], latent_gain)
    fresh_rows = jnp.concatenate([latent_part, latent[:, QL + DL :]], axis=1).astype(jnp.bfloat16)
    every_query, every_fresh = (
        lax.all_gather(query_latent, "dp", axis=0, tiled=True),
        lax.all_gather(fresh_rows, "dp", axis=0, tiled=True),
    )
    query_part = lax.dot_general(
        every_query, query_weight, (((1,), (2,)), ((), ())), preferred_element_type=jnp.float32
    )
    query_part = query_part.astype(jnp.bfloat16).reshape(row_count, local_heads * slice_width)
    step_index = jnp.arange(step_count, dtype=jnp.int32)
    owner_row = (owner_place[:, None] * step_count + step_index[None, :]).reshape(row_count)
    row_index = jnp.arange(row_count, dtype=jnp.int32)
    reorder = (owner_row[None, :] == row_index[:, None]).astype(jnp.bfloat16)
    query_owned = jnp.dot(reorder, query_part, preferred_element_type=jnp.float32).astype(
        jnp.bfloat16
    )
    own_reorder = lax.dynamic_slice_in_dim(reorder, dp_rank * local_rows, local_rows, 0)
    own_fresh = jnp.dot(own_reorder, every_fresh, preferred_element_type=jnp.float32).astype(
        jnp.bfloat16
    )
    own_fresh = own_fresh.reshape(local_requests, step_count, DL + DR)
    arrived = lax.all_to_all(query_owned, "dp", split_axis=0, concat_axis=1, tiled=True)
    arrived = arrived.reshape(local_requests, step_count, dp_count, local_heads, slice_width)
    cache_blocks = latent_cache.reshape(local_requests, context, dp_count, slice_width)
    fresh_blocks = own_fresh.reshape(local_requests, step_count, dp_count, slice_width)
    old_scores = (
        jnp.einsum("usdhc,updc->ushp", arrived, cache_blocks, preferred_element_type=jnp.float32)
        * score_scale
    )
    live_mask = jnp.arange(context, dtype=jnp.int32)[None, :] < cache_length[:, None]
    old_scores = jnp.where(live_mask[:, None, None, :], old_scores, masked_score)
    new_scores = (
        jnp.einsum("usdhc,ukdc->ushk", arrived, fresh_blocks, preferred_element_type=jnp.float32)
        * score_scale
    )
    causal = step_index[None, :] <= step_index[:, None]
    new_scores = jnp.where(causal[None, :, None, :], new_scores, masked_score)
    row_peak = jnp.maximum(jnp.max(old_scores, axis=-1), jnp.max(new_scores, axis=-1))
    old_exp = jnp.exp(old_scores - row_peak[..., None])
    new_exp = jnp.exp(new_scores - row_peak[..., None])
    exp_total = jnp.sum(old_exp, axis=-1) + jnp.sum(new_exp, axis=-1)
    old_weight = (old_exp / exp_total[..., None]).astype(jnp.bfloat16)
    new_weight = (new_exp / exp_total[..., None]).astype(jnp.bfloat16)
    mixed_values = jnp.einsum(
        "ushp,upc->ushc", old_weight, latent_cache[:, :, :DL], preferred_element_type=jnp.float32
    )
    mixed_values = mixed_values + jnp.einsum(
        "ushk,ukc->ushc", new_weight, own_fresh[:, :, :DL], preferred_element_type=jnp.float32
    )
    attended = mixed_values.astype(jnp.bfloat16)
    head_values = jnp.einsum(
        "ushc,hcv->ushv", attended, value_weight, preferred_element_type=jnp.float32
    )
    head_values = head_values.astype(jnp.bfloat16).reshape(local_rows, local_heads * value_width)
    slot_terms = lax.dot_general(
        output_weight,
        lax.all_gather(head_values, "dp", axis=0, tiled=True),
        (((1,), (1,)), ((), ())),
        preferred_element_type=jnp.float32,
    )
    request_terms = jnp.take(slot_terms, owner_row, axis=1)
    block_sum = lax.psum(request_terms, "tp")
    attn_output = lax.all_to_all(
        block_sum.astype(jnp.bfloat16), "dp", split_axis=1, concat_axis=0, tiled=True
    ).astype(block_sum.dtype)
    residual = round_keep(stream + attn_output)
    square_total = jnp.sum(residual * residual, axis=0)
    normed = residual * lax.rsqrt(square_total / D + epsilon)[None, :] * final_gain[:, None]
    normed = normed.astype(jnp.bfloat16)
    whole_normed = lax.all_gather(normed, "dp", axis=1, tiled=True)
    logits = lax.dot_general(
        whole_normed, head_weight, (((0,), (0,)), ((), ())), preferred_element_type=jnp.float32
    )
    vocab_width = head_weight.shape[1]
    vocab_start = (dp_rank * tp_count + tp_rank) * vocab_width
    draft_flat = draft_tokens.reshape(row_count)
    target_hit = (draft_flat - vocab_start)[:, None] == jnp.arange(vocab_width, dtype=jnp.int32)[
        None, :
    ]
    target_part = jnp.sum(jnp.where(target_hit, logits, jnp.zeros_like(logits)), axis=1)
    local_peak = jnp.max(logits, axis=1)
    vocab_peak = lax.pmax(local_peak, ("dp", "tp"))
    shifted_total = jnp.sum(jnp.exp(logits - vocab_peak[:, None]), axis=1)
    vocab_total, target = lax.psum((shifted_total, target_part), ("dp", "tp"))
    log_total = vocab_peak + jnp.log(vocab_total)
    accepted = (step_index[None, :] < accept_length[:, None]).reshape(row_count)
    log_probs = jnp.where(accepted[:, None], logits - log_total[:, None], jnp.zeros_like(logits))
    draft_scores = jnp.where(accepted, target - log_total, jnp.zeros_like(target))
    slot_global = dp_rank * local_requests + jnp.arange(local_requests, dtype=jnp.int32)
    slot_match = owner_place[None, :] == slot_global[:, None]
    slot_accept = jnp.sum(
        jnp.where(slot_match, accept_length[None, :], jnp.zeros_like(slot_match, dtype=jnp.int32)),
        axis=1,
    )
    keep_mask = step_index[None, :, None] < slot_accept[:, None, None]
    committed = jnp.where(keep_mask, own_fresh, jnp.zeros_like(own_fresh))
    return (log_probs, draft_scores, committed)


def solution(mesh):
    return jax.shard_map(
        on_device,
        mesh=mesh,
        in_specs=(
            P(None, "dp"),
            P(),
            P(None, "tp"),
            P(),
            P(),
            P("tp", "dp", None),
            P("dp", None, None),
            P("dp"),
            P(),
            P(),
            P("tp", None, None),
            P("dp", "tp"),
            P(),
            P(None, ("dp", "tp")),
            P(),
        ),
        out_specs=(P(None, ("dp", "tp")), P(), P("dp", None, None)),
        check_vma=False,
    )
```

profile of v0, /device:TPU:32, one launch (start us, length us, event | category | flops | bytes accessed | tf_op | source)
XLA Modules:
  0.0 608.4 jit_solution(11450530921332447881)
XLA Ops:
  7.3 1.2 fusion.38
  8.5 3.4 convolution_bitcast_fusion.1
  11.9 13.3 %all-gather = f32[8,264,16]{1,2,0:T(8,128)S(1)} all-gather(f32[1,264,16]{1,2,0:T(8,128)S(1)} %convolution_bitcast_fusion.1), channel_id=1, replica_groups=mesh['dp'=32,'tp'=8] {'tp'}, dimensions={0}, use_global_device_ids=true | all-gather | bytes 152064 | tf_op jit(solution)/shard_map/all_gather | solution.py:61
  25.6 0.7 multiply_convert_fusion
  26.9 52.0 %all_gather.17 = bf16[512,576]{1,0:T(8,128)(2,1)S(1)} all-gather(bf16[16,576]{1,0:T(8,128)(2,1)S(1)} %pad_maximum_fusion), channel_id=1, replica_groups=mesh['dp'=32,'tp'=8] {'dp'}, dimensions={0}, use_global_device_ids=true | all-gather | bytes 608256 | tf_op jit(solution)/shard_map/all_gather | solution.py:69
  79.8 32.7 %copy.58 = bf16[8,4096,576]{1,0,2:T(8,128)(2,1)} copy(bf16[8,4096,576]{1,2,0:T(8,128)(2,1)} %param.21) | data formatting | bytes 75497472 | tf_op args[6]
  112.6 2.6 fusion.19
  115.2 0.4 convolution_convert_fusion
  115.6 0.9 copy.56
  116.5 7.0 %all-to-all-start = ((bf16[32,16,288]{2,1,0:T(8,128)(2,1)}), bf16[32,16,288]{2,1,0:T(8,128)(2,1)S(1)}, u32[]{:S(2)}, u32[]{:S(2)}) async-start(bf16[32,16,288]{2,1,0:T(8,128)(2,1)} %bitcast.4), calls=%async_computation | async-start | bytes 786432 | tf_op jit(solution)/shard_map/all_to_all | solution.py:87
  123.7 12.2 %all-to-all-done = bf16[32,16,288]{2,1,0:T(8,128)(2,1)S(1)} async-done(((bf16[32,16,288]{2,1,0:T(8,128)(2,1)}), bf16[32,16,288]{2,1,0:T(8,128)(2,1)S(1)}, u32[]{:S(2)}, u32[]{:S(2)}) %all-to-all-start) | async-done | bytes 294944 | tf_op jit(solution)/shard_map/all_to_all | solution.py:87
  135.9 2.2 copy.57
  138.1 2.8 fusion.50
  140.8 71.6 %fusion.8 = (f32[8,2,16]{2,1,0:T(2,128)S(1)}, f32[8,2,16,4096]{3,2,1,0:T(8,128)S(1)}) fusion(pred[8,4096]{1,0:T(8,128)(4,1)S(1)} %iota_compare_fusion.2, bf16[8,4096,32,18,1]{1,0,3,2,4:T(8,128)(2,1)} %bitcast.77, bf16[8,2,32,16,18]{2,1,0,4,3:T(2,128)(2,1)} %bitcast.80), kind=kOutput, calls=%fused_computation.10 | convolution fusion | flops 1211105024 | bytes 42271744 | tf_op jit(solution)/shard_map/usdhc,updc->ushp/dot_general | solution.py:92
  212.6 1.9 copy-done.1
  214.4 1.2 fusion.9
  215.6 15.8 %fusion.2 = f32[8,2,16,512]{3,2,1,0:T(8,128)S(1)} fusion(bf16[8,4096,576]{1,2,0:T(8,128)(2,1)} %param.21, f32[8,2,16,4096]{3,2,1,0:T(8,128)} %copy-done.1, f32[8,2,16]{2,1,0:T(2,128)S(1)} %add.129, f32[8,2,16]{2,1,0:T(2,128)S(1)} %max.9, pred[8,4096]{1,0:T(8,128)(4,1)S(1)} %iota_compare_fusion.2), kind=kOutput, calls=%fused_computation.3 | convolution fusion | flops 1078984704 | bytes 38307840 | tf_op jit(solution)/shard_map/ushp,upc->ushc/dot_general | solution.py:109
  231.7 0.5 fusion.27
  232.2 0.6 copy.102
  233.1 72.2 %all-gather.7.cloned.1.call-done = bf16[512,2048]{1,0:T(8,128)(2,1)} async-done(((bf16[16,2048]{1,0:T(8,128)(2,1)}), bf16[512,2048]{1,0:T(8,128)(2,1)}) %all-gather.7.cloned.1.call-update) | async-done | bytes 2097168 | tf_op jit(solution)/shard_map/all_gather | solution.py:122
  305.3 2.6 convolution_bitcast_fusion
  308.1 1.6 gather_fusion
  309.9 29.2 %all-reduce.2 = bf16[224,512]{0,1:T(8,128)(2,1)S(1)} all-reduce(f32[224,512]{0,1:T(8,128)S(1)} %select_bitcast_fusion), channel_id=1, replica_groups=mesh['dp'=32,'tp'=8] {'tp'}, use_global_device_ids=true, to_apply=%region_7.8 | all-reduce | flops 114688 | bytes 688128 | tf_op jit(solution)/shard_map/psum | solution.py:127
  339.1 17.7 %all_to_all.29 = bf16[224,32,16]{0,2,1:T(8,128)(2,1)S(1)} all-to-all(bf16[224,32,16]{0,2,1:T(8,128)(2,1)S(1)} %bitcast.81), channel_id=1, replica_groups=mesh['dp'=32,'tp'=8] {'dp'}, dimensions={1} | all-to-all | bytes 458752 | tf_op jit(solution)/shard_map/all_to_all | solution.py:128
  357.7 0.8 fusion.36
  359.4 0.7 broadcast_select_fusion
  360.1 85.3 %all-gather.9.cloned.1.call-done = bf16[7168,512]{0,1:T(8,128)(2,1)} async-done(((bf16[7168,16]{0,1:T(8,128)(2,1)}), bf16[7168,512]{0,1:T(8,128)(2,1)}) %all-gather.9.cloned.1.call-update) | async-done | bytes 7340048 | tf_op jit(solution)/shard_map/all_gather | solution.py:135
  445.3 6.2 %fusion.51 = (f32[512]{0:T(512)S(1)}, f32[512,256]{0,1:T(8,128)S(1)}) fusion(bf16[7168,512]{0,1:T(8,128)(2,1)} %all-gather.9.cloned.1.call-done, bf16[7168,256]{1,0:T(8,128)(2,1)} %param.28), kind=kOutput, calls=%fused_computation.95 | convolution fusion | flops 1879178752 | bytes 11536384 | tf_op jit(solution)/shard_map/dot_general | solution.py:136
  451.6 75.0 %pmax.7 = f32[512]{0:T(512)S(1)} all-reduce(f32[512]{0:T(512)S(1)} %get-tuple-element.25), channel_id=1, replica_groups=mesh['dp'=32,'tp'=8] {'dp','tp'}, use_global_device_ids=true, to_apply=%region_10.11 | all-reduce | flops 512 | bytes 4096 | tf_op jit(solution)/shard_map/pmax | solution.py:147
  526.7 73.3 %all-reduce = (f32[512]{0:T(512)S(1)}, f32[512]{0:T(512)S(1)}) all-reduce(f32[512]{0:T(512)S(1)} %get-tuple-element.16, f32[512]{0:T(512)S(1)} %get-tuple-element.15), channel_id=1, replica_groups=mesh['dp'=32,'tp'=8] {'dp','tp'}, use_global_device_ids=true, to_apply=%region_12.13 | all-reduce | flops 1024 | bytes 8192 | tf_op jit(solution)/shard_map/psum | solution.py:149
  600.0 0.6 subtract_select_fusion.1
  600.7 1.0 copy.69
  (75 shorter events, 4.9 us)
Async XLA Ops:
  7.2 224.5 %copy-start = (bf16[16,512,128]{2,1,0:T(8,128)(2,1)S(1)}, bf16[16,512,128]{2,1,0:T(8,128)(2,1)}, u32[]{:S(2)}) copy-start(bf16[16,512,128]{2,1,0:T(8,128)(2,1)} %param.25) | copy-start | bytes 6291460
  7.2 18.4 %copy-start.4 = (f32[1536]{0:T(1024)S(1)}, f32[1536]{0:T(1024)}, u32[]{:S(2)}) copy-start(f32[1536]{0:T(1024)} %param.18) | copy-start | bytes 18436
  7.2 19.2 %copy-start.6 = (s32[256]{0:T(256)S(1)}, s32[256]{0:T(256)}, u32[]{:S(2)}) copy-start(s32[256]{0:T(256)} %param.23) | copy-start | bytes 3076
  7.2 19.6 %copy-start.7 = (f32[512]{0:T(512)S(1)}, f32[512]{0:T(512)}, u32[]{:S(2)}) copy-start(f32[512]{0:T(512)} %param.19) | copy-start | bytes 6148
  7.2 105.3 %all-gather.5.cloned.1.call-start = ((), (), s32[]{:S(2)}) async-start(), calls=%async_computation.2 | async-start | bytes 1622016 | tf_op jit(solution)/shard_map/all_gather | solution.py:68
  112.5 11.1 %copy-start.9 = (s32[8]{0:T(128)S(1)}, s32[8]{0:T(128)}, u32[]{:S(2)}) copy-start(s32[8]{0:T(128)} %param.22) | copy-start | bytes 100
  116.5 19.3 %all-to-all-start = ((bf16[32,16,288]{2,1,0:T(8,128)(2,1)}), bf16[32,16,288]{2,1,0:T(8,128)(2,1)S(1)}, u32[]{:S(2)}, u32[]{:S(2)}) async-start(bf16[32,16,288]{2,1,0:T(8,128)(2,1)} %bitcast.4), calls=%async_computation | async-start | bytes 786432 | tf_op jit(solution)/shard_map/all_to_all | solution.py:87
  123.5 181.8 %all-gather.7.cloned.1.call-start = ((), (), s32[]{:S(2)}) async-start(), calls=%async_computation.3 | async-start | bytes 2162688 | tf_op jit(solution)/shard_map/all_gather | solution.py:122
  212.5 1.9 copy-start.1
  232.9 212.5 %all-gather.9.cloned.1.call-start = ((), (), s32[]{:S(2)}) async-start(), calls=%async_computation.4 | async-start | bytes 7569408 | tf_op jit(solution)/shard_map/all_gather | solution.py:135
  308.1 49.3 %copy-start.2 = (bf16[7168,16]{0,1:T(8,128)(2,1)S(1)}, bf16[7168,16]{0,1:T(8,128)(2,1)}, u32[]{:S(2)}) copy-start(bf16[7168,16]{0,1:T(8,128)(2,1)} %param.15) | copy-start | bytes 688132
  309.7 47.9 %copy-start.3 = (f32[7168]{0:T(1024)S(1)}, f32[7168]{0:T(1024)}, u32[]{:S(2)}) copy-start(f32[7168]{0:T(1024)} %param.27) | copy-start | bytes 86020
  309.7 48.8 %copy-start.5 = (s32[256]{0:T(256)S(1)}, s32[256]{0:T(256)}, u32[]{:S(2)}) copy-start(s32[256]{0:T(256)} %param.24) | copy-start | bytes 3076
  309.7 49.0 %copy-start.8 = (s32[256,2]{0,1:T(2,128)S(1)}, s32[256,2]{0,1:T(2,128)}, u32[]{:S(2)}) copy-start(s32[256,2]{0,1:T(2,128)} %param.29) | copy-start | bytes 6148
Sparse Core Ops, SparseCore 0:
  26.5 78.0 all-gather.4
  233.0 72.2 all-gather.6
  358.6 86.6 all-gather.8
where the time goes:
time: 617 us; the launch traced here: 608 us
  blocking collectives  260 us (42%)
  waiting for transfers between devices  170 us (28%)
  matrix products  106 us (17%)
  local copies, waits for them, and re-layouts  43.3 us (7%)
  between operations  14.4 us (2%)
  starting transfers between devices  7.11 us (1%)
  other arithmetic  7.1 us (1%)
    all_gather x1, waiting for transfers between devices, on_device(): whole_normed = lax.all_gather(normed, 'dp', axis=1, tiled=True)  85.3 us
    pmax x1, blocking collectives, on_device(): vocab_peak = lax.pmax(local_peak, ('dp', 'tp'))  75 us
    psum x1, blocking collectives, on_device(): vocab_total, target = lax.psum((shifted_total, target_part), ('dp', 'tp'))  73.3 us
    all_gather x1, waiting for transfers between devices, on_device(): lax.all_gather(head_values, 'dp', axis=0, tiled=True)  72.2 us
    dot_general x1, matrix products, on_device(): jnp.einsum('usdhc,updc->ushp', arrived, cache_blocks, preferred_element_t...  71.6 us
    all_gather x1, blocking collectives, on_device(): lax.all_gather(fresh_rows, 'dp', axis=0, tiled=True)  52 us
    unnamed x24, local copies, waits for them, and re-layouts  36.4 us
    psum x1, blocking collectives, on_device(): block_sum = lax.psum(request_terms, 'tp')  29.2 us
  transfers between devices with their start and end apart: 4, of which 3 were waited for; matrix products, arithmetic and copies ran while one was open for 6% of the time, Pallas kernels for 0%

commit v1 on v0

v1 whole, which is shorter than its diff:
```python
import jax
import jax.numpy as jnp
from jax import lax
from jax.experimental import pallas as pl
from jax.experimental.pallas import tpu as pltpu
from jax.sharding import Mesh, PartitionSpec as P

D = 7168
QL = 1536
DL = 512
DR = 64
DC = DL + DR
CTX = 4096
NX, NZ, NY, NC = 4, 8, 4, 2
DP = ("x", "z")
TP = ("y", "c")
CHUNK = 1024

epsilon = 1e-06
score_scale = 192.0 ** (-0.5)
masked_score = -1e30


def row_norm(values, gain_vector):
    inverse_rms = lax.rsqrt(jnp.mean(values * values, axis=-1, keepdims=True) + epsilon)
    return values * inverse_rms * gain_vector


def share(block, axes, count):
    copies = jnp.broadcast_to(block[None], (count,) + block.shape)
    return lax.all_to_all(copies, axes, split_axis=0, concat_axis=0, tiled=True)


def swap_cores(block):
    return lax.ppermute(block, "c", [(0, 1), (1, 0)])


def attend_kernel(length_ref, q_ref, fresh_ref, kt_hbm, out_ref, kbuf, sbuf, sems):
    slots, rows, _ = q_ref.shape
    chunks = CTX // CHUNK

    def copy(slot, chunk):
        start = chunk * CHUNK
        if not isinstance(start, int):
            start = pl.multiple_of(start, CHUNK)
        return pltpu.make_async_copy(
            kt_hbm.at[slot, :, pl.ds(start, CHUNK)], kbuf.at[slot, chunk], sems.at[slot, chunk]
        )

    for slot in range(slots):
        for chunk in range(chunks):

            @pl.when(chunk * CHUNK < length_ref[slot])
            def _():
                copy(slot, chunk).start()

    def one_slot(slot, carry):
        length = length_ref[slot]
        live = (length + (CHUNK - 1)) // CHUNK
        q = q_ref[slot]
        fresh = fresh_ref[slot]
        new = lax.dot_general(q, fresh, (((1,), (1,)), ((), ())), preferred_element_type=jnp.float32)
        new = new * score_scale
        key_at = lax.broadcasted_iota(jnp.int32, new.shape, 1)
        step_at = lax.broadcasted_iota(jnp.int32, new.shape, 0) // (rows // 2)
        new = jnp.where(key_at <= step_at, new, masked_score)

        def score(chunk, peak):
            copy(slot, chunk).wait()
            s = jnp.dot(q, kbuf[slot, chunk], preferred_element_type=jnp.float32) * score_scale
            at = chunk * CHUNK + lax.broadcasted_iota(jnp.int32, s.shape, 1)
            s = jnp.where(at < length, s, masked_score)
            sbuf[chunk] = s
            for lane in range(0, CHUNK, 128):
                peak = jnp.maximum(peak, s[:, lane : lane + 128])
            return peak

        peak = lax.fori_loop(0, live, score, jnp.full((rows, 128), masked_score, jnp.float32))
        peak = jnp.maximum(
            jnp.max(peak, axis=-1, keepdims=True), jnp.max(new, axis=-1, keepdims=True)
        )
        new = jnp.exp(new - peak)

        def lift(chunk, total):
            e = jnp.exp(sbuf[chunk] - peak)
            sbuf[chunk] = e
            for lane in range(0, CHUNK, 128):
                total = total + e[:, lane : lane + 128]
            return total

        total = lax.fori_loop(0, live, lift, jnp.zeros((rows, 128), jnp.float32))
        total = jnp.sum(total, axis=-1, keepdims=True) + jnp.sum(new, axis=-1, keepdims=True)
        inverse = 1.0 / total
        mixed = jnp.dot(
            (new * inverse).astype(jnp.bfloat16), fresh[:, :DL], preferred_element_type=jnp.float32
        )

        def mix(chunk, acc):
            weight = (sbuf[chunk] * inverse).astype(jnp.bfloat16)
            return acc + lax.dot_general(
                weight,
                kbuf[slot, chunk, :DL, :],
                (((1,), (1,)), ((), ())),
                preferred_element_type=jnp.float32,
            )

        mixed = lax.fori_loop(0, live, mix, mixed)
        out_ref[slot] = mixed.astype(jnp.bfloat16)
        return carry

    lax.fori_loop(0, slots, one_slot, 0)


def attend(lengths, q, fresh, cache):
    slots, rows, _ = q.shape
    keys = jnp.swapaxes(cache, 1, 2)
    return pl.pallas_call(
        attend_kernel,
        out_shape=jax.ShapeDtypeStruct((slots, rows, DL), jnp.bfloat16),
        grid_spec=pltpu.PrefetchScalarGridSpec(
            num_scalar_prefetch=1,
            grid=(1,),
            in_specs=[
                pl.BlockSpec(q.shape, lambda i, n: (0, 0, 0)),
                pl.BlockSpec(fresh.shape, lambda i, n: (0, 0, 0)),
                pl.BlockSpec(memory_space=pl.ANY),
            ],
            out_specs=pl.BlockSpec((slots, rows, DL), lambda i, n: (0, 0, 0)),
            scratch_shapes=[
                pltpu.VMEM((slots, CTX // CHUNK, DC, CHUNK), jnp.bfloat16),
                pltpu.VMEM((CTX // CHUNK, rows, CHUNK), jnp.float32),
                pltpu.SemaphoreType.DMA((slots, CTX // CHUNK)),
            ],
        ),
        compiler_params=pltpu.CompilerParams(vmem_limit_bytes=44 * 1024 * 1024),
        name="attend",
    )(lengths, q, fresh, keys)


HALF = D // (NX * NZ * NC)


def head_kernel(core_ref, own_ref, other_ref, gain_ref, weight_hbm, out_ref, wbuf, nbuf, sem):
    core = core_ref[0]
    copies = [
        pltpu.make_async_copy(weight_hbm.at[x], wbuf.at[x], sem.at[x]) for x in range(NX)
    ]
    for copy in copies:
        copy.start()
    gain = jnp.transpose(gain_ref[...])
    inverse = []
    for y in range(NY):

        def squares(x, acc):
            for ref in (own_ref, other_ref):
                for z in range(NZ):
                    v = ref[x, y, z].astype(jnp.float32)
                    acc = acc + jnp.sum((v * v).reshape(HALF // 8, 8, 128), axis=0)
            return acc

        acc = lax.fori_loop(0, NX, squares, jnp.zeros((8, 128), jnp.float32))
        inverse.append(lax.rsqrt(jnp.sum(acc, axis=0, keepdims=True) / D + epsilon))
    for x in range(NX):
        copies[x].wait()
        for half, ref in ((core, own_ref), (1 - core, other_ref)):
            for z in range(NZ):
                at = (x * NZ + z) * NC
                column = jnp.where(half == 0, gain[:, at : at + 1], gain[:, at + 1 : at + 2])
                for y in range(NY):
                    v = ref[x, y, z].astype(jnp.float32)
                    nbuf[y, z] = (v * inverse[y] * column).astype(jnp.bfloat16)
            weight = wbuf[x, :, half].reshape(NZ * HALF, wbuf.shape[-1])
            for y in range(NY):
                part = lax.dot_general(
                    nbuf[y].reshape(NZ * HALF, 128),
                    weight,
                    (((0,), (0,)), ((), ())),
                    preferred_element_type=jnp.float32,
                )
                if x == 0 and ref is own_ref:
                    out_ref[y] = part
                else:
                    out_ref[y] += part


def head(core, own, other, gain, weight):
    width = weight.shape[1]
    weight = weight.reshape(NX, NZ, NC, HALF, width)
    vmem = pl.BlockSpec(memory_space=pltpu.VMEM)
    return pl.pallas_call(
        head_kernel,
        out_shape=jax.ShapeDtypeStruct((NY, 128, width), jnp.float32),
        in_specs=[
            pl.BlockSpec(memory_space=pltpu.SMEM),
            vmem,
            vmem,
            vmem,
            pl.BlockSpec(memory_space=pl.ANY),
        ],
        out_specs=vmem,
        scratch_shapes=[
            pltpu.VMEM(weight.shape, jnp.bfloat16),
            pltpu.VMEM((NY, NZ, HALF, 128), jnp.bfloat16),
            pltpu.SemaphoreType.DMA((NX,)),
        ],
        compiler_params=pltpu.CompilerParams(vmem_limit_bytes=32 * 1024 * 1024),
        name="head",
    )(core, own, other, gain.reshape(NX * NZ * NC, HALF), weight)


def merge(peak, total, hit):
    top = jnp.max(peak, axis=0)
    return top, jnp.sum(total * jnp.exp(peak - top[None]), axis=0), jnp.sum(hit, axis=0)


def on_device(
    hidden_state,
    attention_gain,
    down_weight,
    query_gain,
    latent_gain,
    query_weight,
    latent_cache,
    cache_length,
    owner_place,
    accept_length,
    value_weight,
    output_weight,
    final_gain,
    head_weight,
    draft_tokens,
):
    x, z, y, c = (lax.axis_index(a) for a in ("x", "z", "y", "c"))
    d = x * NZ + z
    t = y * NC + c
    dp_count, tp_count = NX * NZ, NY * NC
    request_count, step_count = draft_tokens.shape
    row_count = request_count * step_count
    local_requests = latent_cache.shape[0]
    local_rows = local_requests * step_count
    slice_width = query_weight.shape[1]
    local_heads, _, value_width = value_weight.shape
    own_rows = local_rows // tp_count
    step_index = jnp.arange(step_count, dtype=jnp.int32)

    stream = hidden_state.astype(jnp.float32)
    scaled = (stream * attention_gain[:, None]).astype(jnp.bfloat16)
    column_part = lax.dot_general(
        scaled, down_weight, (((0,), (0,)), ((), ())), preferred_element_type=jnp.float32
    )
    inverse_norm = lax.rsqrt(jnp.sum(stream * stream, axis=0) / D + epsilon)
    column_part = column_part * inverse_norm[:, None]
    latent = lax.all_to_all(
        column_part.reshape(tp_count, own_rows, -1), TP, split_axis=0, concat_axis=0, tiled=True
    )
    latent = jnp.swapaxes(latent, 0, 1).reshape(own_rows, QL + DC)
    query_latent = row_norm(latent[:, :QL], query_gain)
    latent_part = row_norm(latent[:, QL : QL + DL], latent_gain)
    rows = jnp.concatenate([query_latent, latent_part, latent[:, QL + DL :]], axis=1)
    rows = rows.astype(jnp.bfloat16)

    rows = share(rows, "z", NZ).reshape(NZ * own_rows, QL + DC)
    rows = share(rows, ("x", "y"), NX * NY).reshape(row_count // NC, QL + DC)
    other_rows = swap_cores(rows)
    place = jnp.arange(row_count // NC, dtype=jnp.int32)
    at_i = place % own_rows
    at_z = place // own_rows % NZ
    at_y = place // (own_rows * NZ) % NY
    at_x = place // (own_rows * NZ * NY)

    def row_ids(core):
        return ((at_x * NZ + at_z) * tp_count + at_y * NC + core) * own_rows + at_i

    request_row = jnp.concatenate([row_ids(c), row_ids(1 - c)])

    weight = jnp.swapaxes(query_weight, 0, 1).reshape(slice_width * local_heads, QL)

    def project(block):
        part = lax.dot_general(
            block[:, :QL], weight, (((1,), (1,)), ((), ())), preferred_element_type=jnp.float32
        )
        return part.astype(jnp.bfloat16)

    query_part = jnp.concatenate([project(rows), project(other_rows)])
    every_fresh = jnp.concatenate([rows[:, QL:], other_rows[:, QL:]])
    owner_row = (owner_place[:, None] * step_count + step_index[None, :]).reshape(row_count)
    slot_of_place = jnp.zeros((row_count,), jnp.int32)
    row_index = jnp.arange(row_count, dtype=jnp.int32)
    same = request_row[None, :] == row_index[:, None]
    slot_of_place = jnp.sum(jnp.where(same, owner_row[:, None], 0), axis=0)
    reorder = (slot_of_place[None, :] == row_index[:, None]).astype(jnp.bfloat16)
    query_owned = jnp.dot(reorder, query_part, preferred_element_type=jnp.float32)
    query_owned = query_owned.astype(jnp.bfloat16).reshape(dp_count, local_rows, -1)
    own_reorder = (
        slot_of_place[None, :] == (d * local_rows + jnp.arange(local_rows, dtype=jnp.int32))[:, None]
    ).astype(jnp.bfloat16)
    own_fresh = jnp.dot(own_reorder, every_fresh, preferred_element_type=jnp.float32)
    own_fresh = own_fresh.astype(jnp.bfloat16).reshape(local_requests, step_count, DC)

    lane_rows = local_rows // NY
    mine = hidden_state.reshape(dp_count, NC, HALF, NY, lane_rows)
    mine = lax.dynamic_index_in_dim(mine, c, 1, keepdims=False)
    mine = lax.dynamic_index_in_dim(mine, y, 2, keepdims=False)
    mine = mine.reshape(dp_count, local_rows, HALF * lane_rows // local_rows)
    width = slice_width * local_heads
    arrived = lax.all_to_all(
        jnp.concatenate([query_owned, mine], axis=2), DP, split_axis=0, concat_axis=0, tiled=True
    )
    stream_block = arrived[:, :, width:].reshape(dp_count, HALF, lane_rows)
    stream_block = jnp.transpose(stream_block, (1, 0, 2)).reshape(HALF, dp_count * lane_rows)
    arrived = arrived[:, :, :width].reshape(
        dp_count, local_requests, step_count, slice_width, local_heads
    )
    queries = jnp.transpose(arrived, (1, 2, 4, 0, 3)).reshape(
        local_requests, step_count * local_heads, DC
    )

    fresh_padded = jnp.pad(own_fresh, ((0, 0), (0, 16 - step_count), (0, 0)))
    attended = attend(cache_length, queries, fresh_padded, latent_cache)
    attended = attended.reshape(local_requests, step_count, local_heads, DL)
    head_values = jnp.einsum(
        "ushc,hcv->ushv", attended, value_weight, preferred_element_type=jnp.float32
    )
    head_values = head_values.astype(jnp.bfloat16).reshape(local_rows, local_heads * value_width)
    head_values = share(head_values, "z", NZ).reshape(NZ * local_rows, -1)
    head_values = share(head_values, "x", NX).reshape(row_count, -1)

    turned = row_index.reshape(dp_count, NY, lane_rows).swapaxes(0, 1).reshape(row_count)
    turned_owner = owner_row.reshape(dp_count, NY, lane_rows).swapaxes(0, 1).reshape(row_count)
    turn = (turned_owner[:, None] == row_index[None, :]).astype(jnp.bfloat16)
    head_values = jnp.dot(turn, head_values, preferred_element_type=jnp.float32)
    head_values = head_values.astype(jnp.bfloat16)
    terms = lax.dot_general(
        output_weight, head_values, (((1,), (1,)), ((), ())), preferred_element_type=jnp.float32
    )
    terms = terms.reshape(NC, HALF, row_count)
    kept = lax.dynamic_index_in_dim(terms, c, 0, keepdims=False)
    sent = lax.dynamic_index_in_dim(terms, 1 - c, 0, keepdims=False)
    kept = kept + swap_cores(sent)
    kept = jnp.swapaxes(kept.reshape(HALF, NY, row_count // NY), 0, 1)
    kept = lax.all_to_all(kept, "y", split_axis=0, concat_axis=0, tiled=True)
    residual = (jnp.sum(kept, axis=0) + stream_block.astype(jnp.float32)).astype(jnp.bfloat16)

    residual = share(residual, "z", NZ)
    residual = share(residual, ("x", "y"), NX * NY)
    residual = residual.reshape(NX, NY, NZ, HALF, row_count // NY)
    other = swap_cores(residual)
    logits = head(c.reshape(1), residual, other, final_gain, head_weight)

    vocab_width = head_weight.shape[1]
    logits = logits.reshape(row_count, vocab_width)
    vocab_start = (d * tp_count + t) * vocab_width

    def turn_rows(flat):
        return flat.reshape(dp_count, NY, lane_rows).swapaxes(0, 1).reshape(row_count)

    target_hit = (turn_rows(draft_tokens) - vocab_start)[:, None] == jnp.arange(
        vocab_width, dtype=jnp.int32
    )[None, :]
    hit = jnp.sum(jnp.where(target_hit, logits, jnp.zeros_like(logits)), axis=1)
    peak = jnp.max(logits, axis=1)
    total = jnp.sum(jnp.exp(logits - peak[:, None]), axis=1)
    stats = jnp.stack([peak, total, hit]).reshape(3, NY, 128)
    stats = jnp.stack([stats, swap_cores(stats)])
    stats = jnp.stack(merge(stats[:, 0], stats[:, 1], stats[:, 2]))
    stats = share(stats, "y", NY)
    stats = jnp.stack(merge(stats[:, 0], stats[:, 1], stats[:, 2]))
    stats = share(stats, DP, dp_count)
    peak, total, target = merge(stats[:, 0], stats[:, 1], stats[:, 2])
    log_total = (peak + jnp.log(total)).reshape(row_count)
    target = target.reshape(row_count)
    accepted = turn_rows((step_index[None, :] < accept_length[:, None]).reshape(row_count))
    log_probs = jnp.where(accepted[:, None], logits - log_total[:, None], jnp.zeros_like(logits))
    draft_scores = jnp.where(accepted, target - log_total, jnp.zeros_like(target))

    def back(turned_rows):
        shape = turned_rows.shape[1:]
        turned_rows = turned_rows.reshape((NY, dp_count, lane_rows) + shape)
        return jnp.swapaxes(turned_rows, 0, 1).reshape((row_count,) + shape)

    slot_global = d * local_requests + jnp.arange(local_requests, dtype=jnp.int32)
    slot_match = owner_place[None, :] == slot_global[:, None]
    slot_accept = jnp.sum(
        jnp.where(slot_match, accept_length[None, :], jnp.zeros_like(slot_match, dtype=jnp.int32)),
        axis=1,
    )
    keep_mask = step_index[None, :, None] < slot_accept[:, None, None]
    committed = jnp.where(keep_mask, own_fresh, jnp.zeros_like(own_fresh))
    return (back(log_probs), back(draft_scores), committed)


def solution(mesh):
    split = Mesh(mesh.devices.reshape(NX, NZ, NY, NC), ("x", "z", "y", "c"))
    return jax.shard_map(
        on_device,
        mesh=split,
        in_specs=(
            P(None, DP),
            P(),
            P(None, TP),
            P(),
            P(),
            P(TP, DP, None),
            P(DP, None, None),
            P(DP),
            P(),
            P(),
            P(TP, None, None),
            P(DP, TP),
            P(),
            P(None, DP + TP),
            P(),
        ),
        out_specs=(P(None, DP + TP), P(), P(DP, None, None)),
        check_vma=False,
    )
```

time: 617 us -> 297 us (0.48)
  blocking collectives: 260 us -> 126 us
  waiting for transfers between devices: 170 us -> 66.1 us
  matrix products: 106 us -> 11.4 us
  Pallas kernels: 0 us -> 32 us
  starting transfers between devices: 7.11 us -> 22 us
  local copies, waits for them, and re-layouts: 43.3 us -> 28.9 us
  between operations: 14.4 us -> 1.3 us
    all_gather x3 -> x0, waiting for transfers between devices: 157 us -> none  [the longest x1 85.3 us: on_device(): whole_normed = lax.all_gather(normed, 'dp', axis=1, tiled=True)]
    all_to_all x1 -> x6, blocking collectives: 17.7 us -> 126 us  [the longest x5 116 us: share(): return lax.all_to_all(copies, axes, split_axis=0, concat_axis=0, tiled=True)]
    psum x2 -> x0, blocking collectives: 102 us -> none  [the longest x1 73.3 us: on_device(): vocab_total, target = lax.psum((shifted_total, target_part), ('dp', 'tp'))]
    dot_general x7 -> x3, matrix products: 102 us -> 6.2 us  [the longest x2 3.11 us: project(): lax.dot_general(block[:, :QL], weight, (((1,), (1,)), ((), ())), preferre...]
    pmax x1 -> x0, blocking collectives: 75 us -> none  [on_device(): vocab_peak = lax.pmax(local_peak, ('dp', 'tp'))]
    all_gather x2 -> x0, blocking collectives: 65.4 us -> none  [the longest x1 52 us: on_device(): lax.all_gather(fresh_rows, 'dp', axis=0, tiled=True)]
    all_to_all x1 -> x5, waiting for transfers between devices: 12.2 us -> 57.4 us  [the longest x3 37.8 us: share(): return lax.all_to_all(copies, axes, split_axis=0, concat_axis=0, tiled=True)]
    unnamed x24 -> x29, local copies, waits for them, and re-layouts: 36.4 us -> 4.31 us
  transfers between devices with their start and end apart: 4 -> 9, of which waited for: 3 -> 8; matrix products, arithmetic and copies ran while one was open for 6% -> 3% of each run, Pallas kernels for 0% -> 0%
where the time goes in v1:
time: 297 us; the launch traced here: 294 us
  blocking collectives  126 us (42%)
  waiting for transfers between devices  66.1 us (22%)
  Pallas kernels  32 us (11%)
  local copies, waits for them, and re-layouts  28.9 us (10%)
  starting transfers between devices  22 us (7%)
  matrix products  11.4 us (4%)
  other arithmetic  6.2 us (2%)
    all_to_all x5, blocking collectives, share(): return lax.all_to_all(copies, axes, split_axis=0, concat_axis=0, tiled=True)  116 us
    all_to_all x3, waiting for transfers between devices, share(): return lax.all_to_all(copies, axes, split_axis=0, concat_axis=0, tiled=True)  37.8 us
    pallas_call x1, Pallas kernels, attend(): pl.pallas_call(attend_kernel, out_shape=jax.ShapeDtypeStruct((slots, rows...  21.7 us
    all_to_all x1, waiting for transfers between devices, on_device(): lax.all_to_all(jnp.concatenate([query_owned, mine], axis=2), DP, split_ax...  14.3 us
    all_to_all x3, starting transfers between devices, share(): return lax.all_to_all(copies, axes, split_axis=0, concat_axis=0, tiled=True)  12.4 us
    pallas_call x1, Pallas kernels, head(): pl.pallas_call(head_kernel, out_shape=jax.ShapeDtypeStruct((NY, 128, widt...  10.2 us
    all_to_all x1, blocking collectives, on_device(): lax.all_to_all(column_part.reshape(tp_count, own_rows, -1), TP, split_axi...  9.67 us
    ppermute x4, waiting for transfers between devices, swap_cores(): return lax.ppermute(block, 'c', [(0, 1), (1, 0)])  8.67 us
  transfers between devices with their start and end apart: 9, of which 8 were waited for; matrix products, arithmetic and copies ran while one was open for 3% of the time, Pallas kernels for 0%

profile of v1, /device:TPU:32, one launch (start us, length us, event | category | flops | bytes accessed | tf_op | source)
XLA Modules:
  0.0 293.6 jit_solution(12323893429701530814)
XLA Ops:
  1.9 3.4 %convolution_multiply_fusion = f32[16,264]{1,0:T(8,128)S(1)} fusion(bf16[7168,264]{0,1:T(8,128)(2,1)} %param.17, bf16[7168,16]{0,1:T(8,128)(2,1)} %param.15, f32[7168]{0:T(1024)} %param.16, f32[16]{0:T(128)S(1)} %add_rsqrt_fusion.2), kind=kOutput, calls=%fused_computation.9 | convolution fusion | flops 60903552 | bytes 4059712 | tf_op jit(solution)/shard_map/dot_general | solution.py:248
  5.4 9.7 %all_to_all.55 = f32[8,2,264]{2,1,0:T(2,128)S(1)} all-to-all(f32[8,2,264]{2,1,0:T(2,128)S(1)} %reshape.287), channel_id=1, replica_groups=mesh['x'=4,'z'=8,'y'=4,'c'=2] {'y','c'}, dimensions={0} | all-to-all | bytes 33792 | tf_op jit(solution)/shard_map/all_to_all | solution.py:253
  15.7 15.3 %all_to_all.56 = bf16[8,2,2112]{2,1,0:T(2,128)(2,1)S(1)} all-to-all(bf16[8,2,2112]{2,1,0:T(2,128)(2,1)S(1)} %broadcast_in_dim.58), channel_id=1, replica_groups=mesh['x'=4,'z'=8,'y'=4,'c'=2] {'z'}, dimensions={0} | all-to-all | bytes 135168 | tf_op jit(solution)/shard_map/all_to_all | solution.py:31
  31.2 21.4 %all_to_all.57 = bf16[16,16,2112]{2,1,0:T(8,128)(2,1)S(1)} all-to-all(bf16[16,16,2112]{2,1,0:T(8,128)(2,1)S(1)} %broadcast_in_dim.60), channel_id=1, replica_groups=mesh['x'=4,'z'=8,'y'=4,'c'=2] {'x','y'}, dimensions={0} | all-to-all | bytes 2162688 | tf_op jit(solution)/shard_map/all_to_all | solution.py:31
  52.5 1.4 copy.196
  56.8 1.6 convolution_convert_fusion.3
  58.5 1.5 convolution_convert_fusion.2
  61.1 1.9 copy.197
  63.0 1.9 pad_maximum_fusion
  64.8 5.6 %all-to-all-start.3 = ((bf16[32,16,316]{2,1,0:T(8,128)(2,1)}), bf16[32,16,316]{2,1,0:T(8,128)(2,1)}, u32[]{:S(2)}, u32[]{:S(2)}) async-start(bf16[32,16,316]{2,1,0:T(8,128)(2,1)} %pad_maximum_fusion), calls=%async_computation.3 | async-start | bytes 786432 | tf_op jit(solution)/shard_map/all_to_all | solution.py:306
  72.0 14.3 %all-to-all-done.3 = bf16[32,16,316]{2,1,0:T(8,128)(2,1)} async-done(((bf16[32,16,316]{2,1,0:T(8,128)(2,1)}), bf16[32,16,316]{2,1,0:T(8,128)(2,1)}, u32[]{:S(2)}, u32[]{:S(2)}) %all-to-all-start.3) | async-done | bytes 323616 | tf_op jit(solution)/shard_map/all_to_all | solution.py:306
  86.4 1.6 copy.229
  88.0 3.5 %copy.201 = bf16[8,2,16,32,18]{4,3,2,1,0:T(8,128)(2,1)} copy(bf16[8,2,16,32,18]{3,2,4,1,0:T(8,128)(2,1)S(1)} %bitcast.132) | data formatting | bytes 589824 | tf_op jit(solution)/shard_map/transpose | solution.py:314
  91.5 4.5 %reshape.295.q_ref = bf16[8,32,576]{2,1,0:T(8,128)(2,1)S(1)} reshape(bf16[8,2,16,32,18]{4,3,2,1,0:T(8,128)(2,1)} %copy.201) | data formatting | bytes 589824 | tf_op jit(solution)/shard_map/reshape | solution.py:314
  96.0 21.7 %attend.1 = bf16[8,32,512]{2,1,0:T(8,128)(2,1)S(1)} custom-call(s32[8]{0:T(128)S(1)} %copy-done.3, bf16[8,32,576]{2,1,0:T(8,128)(2,1)S(1)} %reshape.295.q_ref, bf16[8,16,576]{2,1,0:T(8,128)(2,1)S(1)} %pad.4.fresh_ref, bf16[8,576,4096]{2,1,0:T(8,128)(2,1)} %bitcast.128), custom_call_target="tpu_custom_call" | custom-call | tf_op jit(solution)/shard_map/attend/pallas_call | solution.py:117
  118.3 19.5 %all_to_all.58 = bf16[8,16,2048]{2,1,0:T(8,128)(2,1)S(1)} all-to-all(bf16[8,16,2048]{2,1,0:T(8,128)(2,1)S(1)} %broadcast_in_dim.62), channel_id=1, replica_groups=mesh['x'=4,'z'=8,'y'=4,'c'=2] {'z'}, dimensions={0} | all-to-all | bytes 1048576 | tf_op jit(solution)/shard_map/all_to_all | solution.py:31
  137.8 1.6 broadcast_in_dim.64
  139.4 3.6 %all-to-all-start.5 = ((bf16[4,128,2048]{2,1,0:T(8,128)(2,1)}), bf16[4,128,2048]{2,1,0:T(8,128)(2,1)S(1)}, u32[]{:S(2)}, u32[]{:S(2)}) async-start(bf16[4,128,2048]{2,1,0:T(8,128)(2,1)} %broadcast_in_dim.64), calls=%async_computation.5 | async-start | bytes 4194304 | tf_op jit(solution)/shard_map/all_to_all | solution.py:31
  143.7 23.5 %all-to-all-done.5 = bf16[4,128,2048]{2,1,0:T(8,128)(2,1)S(1)} async-done(((bf16[4,128,2048]{2,1,0:T(8,128)(2,1)}), bf16[4,128,2048]{2,1,0:T(8,128)(2,1)S(1)}, u32[]{:S(2)}, u32[]{:S(2)}) %all-to-all-start.5) | async-done | bytes 2097184 | tf_op jit(solution)/shard_map/all_to_all | solution.py:31
  167.2 3.1 %fusion.8 = f32[512,224]{0,1:T(8,128)S(1)} fusion(bf16[224,2048]{1,0:T(8,128)(2,1)} %param.26, bf16[512,2048]{1,0:T(8,128)(2,1)S(1)} %bitcast.134, s32[512]{0:T(512)S(1)} %eq.43), kind=kOutput, calls=%fused_computation.10 | convolution fusion | flops 1544814592 | bytes 3475456 | tf_op jit(solution)/shard_map/dot_general | solution.py:333
  170.7 1.5 collective-permute-done.1
  173.0 3.4 %all-to-all-start.6 = ((f32[4,112,128]{2,1,0:T(8,128)}), f32[4,112,128]{2,1,0:T(8,128)S(1)}, u32[]{:S(2)}, u32[]{:S(2)}) async-start(f32[4,112,128]{2,1,0:T(8,128)} %copy.205), calls=%async_computation.6 | async-start | bytes 458752 | tf_op jit(solution)/shard_map/all_to_all | solution.py:341
  177.9 5.3 %all-to-all-done.6 = f32[4,112,128]{2,1,0:T(8,128)S(1)} async-done(((f32[4,112,128]{2,1,0:T(8,128)}), f32[4,112,128]{2,1,0:T(8,128)S(1)}, u32[]{:S(2)}, u32[]{:S(2)}) %all-to-all-start.6) | async-done | bytes 229408 | tf_op jit(solution)/shard_map/all_to_all | solution.py:341
  183.3 13.7 %all_to_all.59 = bf16[8,112,128]{2,1,0:T(8,128)(2,1)S(1)} all-to-all(bf16[8,112,128]{2,1,0:T(8,128)(2,1)S(1)} %broadcast_in_dim.65), channel_id=1, replica_groups=mesh['x'=4,'z'=8,'y'=4,'c'=2] {'z'}, dimensions={0} | all-to-all | bytes 458752 | tf_op jit(solution)/shard_map/all_to_all | solution.py:31
  197.7 46.2 %all_to_all.60 = bf16[16,8,112,128]{3,2,1,0:T(8,128)(2,1)} all-to-all(bf16[16,8,112,128]{3,2,1,0:T(8,128)(2,1)S(1)} %broadcast_in_dim.69), channel_id=1, replica_groups=mesh['x'=4,'z'=8,'y'=4,'c'=2] {'x','y'}, dimensions={0} | all-to-all | bytes 7340032 | tf_op jit(solution)/shard_map/all_to_all | solution.py:31
  244.4 6.3 %collective-permute-done.2.other_ref = bf16[4,4,8,112,128]{4,3,2,1,0:T(8,128)(2,1)} collective-permute-done((bf16[4,4,8,112,128]{4,3,2,1,0:T(8,128)(2,1)}, bf16[4,4,8,112,128]{4,3,2,1,0:T(8,128)(2,1)}, u32[]{:S(2)}, u32[]{:S(2)}) %collective-permute-start.2) | collective-permute-done | bytes 3670048 | tf_op jit(solution)/shard_map/ppermute | solution.py:35
  250.7 2.0 copy-done.2
  252.7 10.2 %head.1 = f32[4,128,256]{2,1,0:T(8,128)S(1)} custom-call(s32[1]{0:T(128)} %bitcast.2.core_ref, bf16[4,4,8,112,128]{4,3,2,1,0:T(8,128)(2,1)} %bitcast.28.own_ref, bf16[4,4,8,112,128]{4,3,2,1,0:T(8,128)(2,1)} %collective-permute-done.2.other_ref, f32[64,112]{1,0:T(8,128)S(1)} %reshape.302.gain_ref, bf16[4,8,2,112,256]{4,3,2,1,0:T(8,128)(2,1)S(1)} %bitcast.126), custom_call_target="tpu_custom_call" | custom-call | tf_op jit(solution)/shard_map/head/pallas_call | solution.py:190
  265.5 3.3 %all-to-all-start.9 = ((f32[4,3,4,128]{3,2,1,0:T(4,128)}), f32[4,3,4,128]{3,2,1,0:T(4,128)S(1)}, u32[]{:S(2)}, u32[]{:S(2)}) async-start(f32[4,3,4,128]{3,2,1,0:T(4,128)} %broadcast_in_dim.70), calls=%async_computation.9 | async-start | bytes 49152 | tf_op jit(solution)/shard_map/all_to_all | solution.py:31
  269.2 4.9 %all-to-all-done.9 = f32[4,3,4,128]{3,2,1,0:T(4,128)S(1)} async-done(((f32[4,3,4,128]{3,2,1,0:T(4,128)}), f32[4,3,4,128]{3,2,1,0:T(4,128)S(1)}, u32[]{:S(2)}, u32[]{:S(2)}) %all-to-all-start.9) | async-done | bytes 24608 | tf_op jit(solution)/shard_map/all_to_all | solution.py:31
  274.9 5.5 %all-to-all-start.10 = ((f32[32,3,4,128]{3,2,1,0:T(4,128)}), f32[32,3,4,128]{3,2,1,0:T(4,128)S(1)}, u32[]{:S(2)}, u32[]{:S(2)}) async-start(f32[32,3,4,128]{3,2,1,0:T(4,128)} %broadcast_in_dim.71), calls=%async_computation.10 | async-start | bytes 393216 | tf_op jit(solution)/shard_map/all_to_all | solution.py:31
  281.3 9.4 %all-to-all-done.10 = f32[32,3,4,128]{3,2,1,0:T(4,128)S(1)} async-done(((f32[32,3,4,128]{3,2,1,0:T(4,128)}), f32[32,3,4,128]{3,2,1,0:T(4,128)S(1)}, u32[]{:S(2)}, u32[]{:S(2)}) %all-to-all-start.10) | async-done | bytes 196640 | tf_op jit(solution)/shard_map/all_to_all | solution.py:31
  (133 shorter events, 20.1 us)
Async XLA Ops:
  0.6 117.1 %copy-start = (bf16[16,512,128]{2,1,0:T(8,128)(2,1)S(1)}, bf16[16,512,128]{2,1,0:T(8,128)(2,1)}, u32[]{:S(2)}) copy-start(bf16[16,512,128]{2,1,0:T(8,128)(2,1)} %param.25) | copy-start | bytes 6291460
  1.9 13.5 %copy-start.6 = (f32[1536]{0:T(1024)S(1)}, f32[1536]{0:T(1024)}, u32[]{:S(2)}) copy-start(f32[1536]{0:T(1024)} %param.18) | copy-start | bytes 18436
  1.9 13.6 %copy-start.9 = (f32[512]{0:T(512)S(1)}, f32[512]{0:T(512)}, u32[]{:S(2)}) copy-start(f32[512]{0:T(512)} %param.19) | copy-start | bytes 6148
  31.1 22.8 %copy-start.8 = (s32[256]{0:T(256)S(1)}, s32[256]{0:T(256)}, u32[]{:S(2)}) copy-start(s32[256]{0:T(256)} %param.23) | copy-start | bytes 3076
  31.1 22.8 %copy-start.4 = (bf16[7168,16]{0,1:T(8,128)(2,1)S(1)}, bf16[7168,16]{0,1:T(8,128)(2,1)}, u32[]{:S(2)}) copy-start(bf16[7168,16]{0,1:T(8,128)(2,1)} %param.15) | copy-start | bytes 688132
  53.9 4.5 %collective-permute-start = (bf16[256,2112]{0,1:T(8,128)(2,1)}, bf16[256,2112]{0,1:T(8,128)(2,1)}, u32[]{:S(2)}, u32[]{:S(2)}) collective-permute-start(bf16[256,2112]{0,1:T(8,128)(2,1)} %copy.196), channel_id=1, source_target_pairs={{0,1},{1,0},{2,3},{3,2},{4,5},{5,4},{6,7},{7,6},{8,9},{9,8},{10,11... | collective-permute-start | bytes 3244040 | tf_op jit(solution)/shard_map/ppermute | solution.py:35
  56.6 1.9 copy-start.11
  64.8 21.5 %all-to-all-start.3 = ((bf16[32,16,316]{2,1,0:T(8,128)(2,1)}), bf16[32,16,316]{2,1,0:T(8,128)(2,1)}, u32[]{:S(2)}, u32[]{:S(2)}) async-start(bf16[32,16,316]{2,1,0:T(8,128)(2,1)} %pad_maximum_fusion), calls=%async_computation.3 | async-start | bytes 786432 | tf_op jit(solution)/shard_map/all_to_all | solution.py:306
  88.0 8.0 %copy-start.3 = (s32[8]{0:T(128)S(1)}, s32[8]{0:T(128)}, u32[]{:S(2)}) copy-start(s32[8]{0:T(128)} %length_ref.1) | copy-start | bytes 100
  139.4 27.8 %all-to-all-start.5 = ((bf16[4,128,2048]{2,1,0:T(8,128)(2,1)}), bf16[4,128,2048]{2,1,0:T(8,128)(2,1)S(1)}, u32[]{:S(2)}, u32[]{:S(2)}) async-start(bf16[4,128,2048]{2,1,0:T(8,128)(2,1)} %broadcast_in_dim.64), calls=%async_computation.5 | async-start | bytes 4194304 | tf_op jit(solution)/shard_map/all_to_all | solution.py:31
  170.4 1.8 collective-permute-start.1
  173.0 10.3 %all-to-all-start.6 = ((f32[4,112,128]{2,1,0:T(8,128)}), f32[4,112,128]{2,1,0:T(8,128)S(1)}, u32[]{:S(2)}, u32[]{:S(2)}) async-start(f32[4,112,128]{2,1,0:T(8,128)} %copy.205), calls=%async_computation.6 | async-start | bytes 458752 | tf_op jit(solution)/shard_map/all_to_all | solution.py:341
  197.7 46.2 %copy-start.5 = (f32[7168]{0:T(1024)S(1)}, f32[7168]{0:T(1024)}, u32[]{:S(2)}) copy-start(f32[7168]{0:T(1024)} %param.27) | copy-start | bytes 86020
  197.7 46.3 %copy-start.10 = (s32[256,2]{0,1:T(2,128)S(1)}, s32[256,2]{0,1:T(2,128)}, u32[]{:S(2)}) copy-start(s32[256,2]{0,1:T(2,128)} %param.29) | copy-start | bytes 6148
  243.9 6.8 %collective-permute-start.2 = (bf16[4,4,8,112,128]{4,3,2,1,0:T(8,128)(2,1)}, bf16[4,4,8,112,128]{4,3,2,1,0:T(8,128)(2,1)}, u32[]{:S(2)}, u32[]{:S(2)}) collective-permute-start(bf16[4,4,8,112,128]{4,3,2,1,0:T(8,128)(2,1)} %bitcast.28.own_ref), channel_id=1, source_target_pairs={{0,1},{1,0},{2,3},{3,2},{4,5},{5,4},{6,7},{7,6},{8,9},{9,8},{10,11... | collective-permute-start | bytes 11010056 | tf_op jit(solution)/shard_map/ppermute | solution.py:35
  250.7 2.0 copy-start.2
  252.7 16.0 %copy-start.7 = (s32[256]{0:T(256)S(1)}, s32[256]{0:T(256)}, u32[]{:S(2)}) copy-start(s32[256]{0:T(256)} %param.24) | copy-start | bytes 3076
  263.5 1.3 collective-permute-start.3
  265.5 8.6 %all-to-all-start.9 = ((f32[4,3,4,128]{3,2,1,0:T(4,128)}), f32[4,3,4,128]{3,2,1,0:T(4,128)S(1)}, u32[]{:S(2)}, u32[]{:S(2)}) async-start(f32[4,3,4,128]{3,2,1,0:T(4,128)} %broadcast_in_dim.70), calls=%async_computation.9 | async-start | bytes 49152 | tf_op jit(solution)/shard_map/all_to_all | solution.py:31
  274.9 15.8 %all-to-all-start.10 = ((f32[32,3,4,128]{3,2,1,0:T(4,128)}), f32[32,3,4,128]{3,2,1,0:T(4,128)S(1)}, u32[]{:S(2)}, u32[]{:S(2)}) async-start(f32[32,3,4,128]{3,2,1,0:T(4,128)} %broadcast_in_dim.71), calls=%async_computation.10 | async-start | bytes 393216 | tf_op jit(solution)/shard_map/all_to_all | solution.py:31
  281.1 12.5 %copy-start.1 = (bf16[16,512,128]{2,1,0:T(8,128)(2,1)S(1)}, bf16[16,512,128]{2,1,0:T(8,128)(2,1)}, u32[]{:S(2)}) copy-start(bf16[16,512,128]{2,1,0:T(8,128)(2,1)} %param.25) | copy-start | bytes 6291460

commit v2 on v1

--- a/solution.py
+++ b/solution.py
@@ -15,6 +15,8 @@
 DP = ("x", "z")
 TP = ("y", "c")
 CHUNK = 1024
+PAD = 64
+REL = (0, 3, 1, 2)
 
 epsilon = 1e-06
 score_scale = 192.0 ** (-0.5)
@@ -35,9 +37,23 @@
     return lax.ppermute(block, "c", [(0, 1), (1, 0)])
 
 
-def attend_kernel(length_ref, q_ref, fresh_ref, kt_hbm, out_ref, kbuf, sbuf, sems):
-    slots, rows, _ = q_ref.shape
+def shift(block, axis, step):
+    return lax.ppermute(block, axis, [(i, (i + step) % 4) for i in range(4)])
+
+
+def ring(block, axis):
+    half = block.shape[0] // 2
+    before = shift(block, axis, 1)
+    after = shift(block, axis, -1)
+    return block, before, after, shift(before[:half], axis, 1), shift(after[half:], axis, -1)
+
+
+def attend_kernel(length_ref, xt_ref, fresh_ref, kt_hbm, out_ref, kbuf, sbuf, qbuf, sems):
+    slots, rows, _ = out_ref.shape
     chunks = CTX // CHUNK
+    row_count, packed, sources = xt_ref.shape
+    heads = slots * rows // row_count
+    width = packed // heads
 
     def copy(slot, chunk):
         start = chunk * CHUNK
@@ -54,10 +70,23 @@
             def _():
                 copy(slot, chunk).start()
 
+    pieces = [
+        xt_ref[:, w * heads : (w + 1) * heads, :].reshape(slots * rows, sources)
+        for w in range(width)
+    ]
+    source = lax.broadcasted_iota(jnp.int32, (DC, DC), 0)
+    target = lax.broadcasted_iota(jnp.int32, (DC, DC), 1)
+    order = target == (source % sources) * width + source // sources
+    order = jnp.where(order, 1.0, 0.0).astype(jnp.bfloat16)
+    q_all = jnp.dot(
+        jnp.concatenate(pieces, axis=1), order, preferred_element_type=jnp.float32
+    ).astype(jnp.bfloat16)
+    qbuf[...] = q_all.reshape(slots, rows, DC)
+
     def one_slot(slot, carry):
         length = length_ref[slot]
         live = (length + (CHUNK - 1)) // CHUNK
-        q = q_ref[slot]
+        q = qbuf[slot]
         fresh = fresh_ref[slot]
         new = lax.dot_general(q, fresh, (((1,), (1,)), ((), ())), preferred_element_type=jnp.float32)
         new = new * score_scale
@@ -111,8 +140,9 @@
     lax.fori_loop(0, slots, one_slot, 0)
 
 
-def attend(lengths, q, fresh, cache):
-    slots, rows, _ = q.shape
+def attend(lengths, packed, fresh, cache):
+    slots = cache.shape[0]
+    rows = packed.shape[0] * (packed.shape[1] * packed.shape[2] // DC) // slots
     keys = jnp.swapaxes(cache, 1, 2)
     return pl.pallas_call(
         attend_kernel,
@@ -121,7 +151,7 @@
             num_scalar_prefetch=1,
             grid=(1,),
             in_specs=[
-                pl.BlockSpec(q.shape, lambda i, n: (0, 0, 0)),
+                pl.BlockSpec(packed.shape, lambda i, n: (0, 0, 0)),
                 pl.BlockSpec(fresh.shape, lambda i, n: (0, 0, 0)),
                 pl.BlockSpec(memory_space=pl.ANY),
             ],
@@ -129,83 +159,172 @@
             scratch_shapes=[
                 pltpu.VMEM((slots, CTX // CHUNK, DC, CHUNK), jnp.bfloat16),
                 pltpu.VMEM((CTX // CHUNK, rows, CHUNK), jnp.float32),
+                pltpu.VMEM((slots, rows, DC), jnp.bfloat16),
                 pltpu.SemaphoreType.DMA((slots, CTX // CHUNK)),
             ],
         ),
-        compiler_params=pltpu.CompilerParams(vmem_limit_bytes=44 * 1024 * 1024),
+        compiler_params=pltpu.CompilerParams(vmem_limit_bytes=46 * 1024 * 1024),
         name="attend",
-    )(lengths, q, fresh, keys)
+    )(lengths, packed, fresh, keys)
 
 
 HALF = D // (NX * NZ * NC)
 
 
-def head_kernel(core_ref, own_ref, other_ref, gain_ref, weight_hbm, out_ref, wbuf, nbuf, sem):
-    core = core_ref[0]
-    copies = [
-        pltpu.make_async_copy(weight_hbm.at[x], wbuf.at[x], sem.at[x]) for x in range(NX)
-    ]
-    for copy in copies:
-        copy.start()
-    gain = jnp.transpose(gain_ref[...])
+PIECES = 5
+
+
+def piece_of(refs, k, m, group):
+    outer, inner = (m, k) if group == 0 else (k, m)
+    refs = refs[group * PIECES : (group + 1) * PIECES]
+    if outer < 3:
+        return refs[outer], inner
+    if inner < 2:
+        return refs[3], inner
+    return refs[4], inner - 2
+
+
+def head_kernel(place_ref, gain_ref, weight_hbm, other_hbm, *rest):
+    refs, rest = rest[: 2 * PIECES], rest[2 * PIECES :]
+    out_ref, wbuf, abuf, bbuf, nbuf, wsem, sem = rest
+    x0, y0, core = place_ref[0], place_ref[1], place_ref[2]
+    bufs = abuf, bbuf
+
+    def block_copy(group, k, m):
+        ref, at = piece_of(refs, k, m, group)
+        return pltpu.make_async_copy(ref.at[at], bufs[group].at[k, m], sem.at[group, k, m])
+
+    def weight_copies(k):
+        at = (x0 + REL[k]) % NX
+        return (
+            pltpu.make_async_copy(weight_hbm.at[at, :, core], wbuf.at[k, 0], wsem.at[k, 0]),
+            pltpu.make_async_copy(other_hbm.at[at], wbuf.at[k, 1], wsem.at[k, 1]),
+        )
+
+    for k in range(NX):
+        for m in range(NY):
+            block_copy(0, k, m).start()
+    for k in range(NX):
+        for m in range(NY):
+            block_copy(1, k, m).start()
+        for copy in weight_copies(k):
+            copy.start()
+    for k in range(NX):
+        for m in range(NY):
+            block_copy(0, k, m).wait()
     inverse = []
-    for y in range(NY):
-
-        def squares(x, acc):
-            for ref in (own_ref, other_ref):
-                for z in range(NZ):
-                    v = ref[x, y, z].astype(jnp.float32)
-                    acc = acc + jnp.sum((v * v).reshape(HALF // 8, 8, 128), axis=0)
-            return acc
-
-        acc = lax.fori_loop(0, NX, squares, jnp.zeros((8, 128), jnp.float32))
-        inverse.append(lax.rsqrt(jnp.sum(acc, axis=0, keepdims=True) / D + epsilon))
-    for x in range(NX):
-        copies[x].wait()
-        for half, ref in ((core, own_ref), (1 - core, other_ref)):
-            for z in range(NZ):
-                at = (x * NZ + z) * NC
-                column = jnp.where(half == 0, gain[:, at : at + 1], gain[:, at + 1 : at + 2])
-                for y in range(NY):
-                    v = ref[x, y, z].astype(jnp.float32)
-                    nbuf[y, z] = (v * inverse[y] * column).astype(jnp.bfloat16)
-            weight = wbuf[x, :, half].reshape(NZ * HALF, wbuf.shape[-1])
-            for y in range(NY):
-                part = lax.dot_general(
-                    nbuf[y].reshape(NZ * HALF, 128),
+    for m in range(NY):
+        total = jnp.zeros((16, 128), jnp.float32)
+        for k in range(NX):
+            total = total + abuf[k, m, NZ // 2 * HALF :, :].astype(jnp.float32)
+        inverse.append(lax.rsqrt(jnp.sum(total, axis=0, keepdims=True) / D + epsilon))
+    for k in range(NX):
+        gain = jnp.transpose(gain_ref[(x0 + REL[k]) % NX, core])
+        for m in range(NY):
+            block_copy(1, k, m).wait()
+        for z in range(NZ):
+            column = gain[:, z : z + 1]
+            at = z % (NZ // 2) * HALF
+            for m in range(NY):
+                v = bufs[z // (NZ // 2)][k, m, at : at + HALF, :].astype(jnp.float32)
+                nbuf[k % 2, m, z] = (v * inverse[m] * column).astype(jnp.bfloat16)
+        for copy in weight_copies(k):
+            copy.wait()
+        for part in range(NC):
+            weight = wbuf[k, part].reshape(NZ * HALF, wbuf.shape[-1])
+            for m in range(NY):
+                term = lax.dot_general(
+                    nbuf[k % 2, m].reshape(NZ * HALF, 128),
                     weight,
                     (((0,), (0,)), ((), ())),
                     preferred_element_type=jnp.float32,
                 )
-                if x == 0 and ref is own_ref:
-                    out_ref[y] = part
+                at = (y0 + REL[m]) % NY
+                if k == 0:
+                    out_ref[part, at] = term
                 else:
-                    out_ref[y] += part
-
-
-def head(core, own, other, gain, weight):
-    width = weight.shape[1]
-    weight = weight.reshape(NX, NZ, NC, HALF, width)
+                    out_ref[part, at] += term
+
+
+def head(place, gain, weight, other, pieces):
+    width = weight.shape[-1]
+    vmem = pl.BlockSpec(memory_space=pltpu.VMEM)
+    far = pl.BlockSpec(memory_space=pltpu.HBM)
+    gain = jnp.transpose(gain.reshape(NX, NZ, NC, HALF), (0, 2, 1, 3))
+    return pl.pallas_call(
+        head_kernel,
+        out_shape=jax.ShapeDtypeStruct((NC, NY, 128, width), jnp.float32),
+        in_specs=[pl.BlockSpec(memory_space=pltpu.SMEM), vmem, far, far] + [far] * len(pieces),
+        out_specs=vmem,
+        scratch_shapes=[
+            pltpu.VMEM((NX, NC, NZ, HALF, width), jnp.bfloat16),
+            pltpu.VMEM((NX, NY) + pieces[0].shape[1:], jnp.bfloat16),
+            pltpu.VMEM((NX, NY) + pieces[PIECES].shape[1:], jnp.bfloat16),
+            pltpu.VMEM((2, NY, NZ, HALF, 128), jnp.bfloat16),
+            pltpu.SemaphoreType.DMA((NX, NC)),
+            pltpu.SemaphoreType.DMA((2, NX, NY)),
+        ],
+        compiler_params=pltpu.CompilerParams(vmem_limit_bytes=60 * 1024 * 1024),
+        name="head",
+    )(place, gain, weight, other, *pieces)
+
+
+def project_kernel(
+    slot_ref, mine_ref, rows_ref, other_ref, weight_ref, stream_ref, out_ref, fresh_ref
+):
+    count = slot_ref.shape[1]
+    half = count // NC
+    width = weight_ref.shape[0]
+    total = None
+    fresh = None
+    for part, ref in enumerate((rows_ref, other_ref)):
+        term = lax.dot_general(
+            ref[:, :QL], weight_ref[...], (((1,), (1,)), ((), ())),
+            preferred_element_type=jnp.float32,
+        ).astype(jnp.bfloat16)
+        slot = slot_ref[:, part * half : (part + 1) * half]
+        wanted = lax.broadcasted_iota(jnp.int32, (count, half), 0)
+        pick = jnp.where(slot == wanted, 1.0, 0.0).astype(jnp.bfloat16)
+        term = jnp.dot(pick, term, preferred_element_type=jnp.float32)
+        total = term if total is None else total + term
+        local = fresh_ref.shape[0]
+        wanted = lax.broadcasted_iota(jnp.int32, (local, half), 0) + mine_ref[0]
+        pick = jnp.where(slot == wanted, 1.0, 0.0).astype(jnp.bfloat16)
+        term = jnp.dot(pick, ref[:, QL : QL + DC], preferred_element_type=jnp.float32)
+        fresh = term if fresh is None else fresh + term
+    fresh_ref[...] = fresh.astype(jnp.bfloat16)
+    out_ref[:, :width] = total.astype(jnp.bfloat16)
+    local = fresh_ref.shape[0]
+    lane_rows = local // NY
+    piece = HALF // NY
+    hidden = stream_ref[...].astype(jnp.float32)
+    chosen = hidden[:lane_rows]
+    for y in range(1, NY):
+        chosen = jnp.where(mine_ref[1] == y, hidden[y * lane_rows : (y + 1) * lane_rows], chosen)
+    for dest in range(NX * NZ):
+        at = dest * NC * HALF
+        wide = jnp.where(
+            mine_ref[2] == 0, chosen[:, at : at + HALF], chosen[:, at + HALF : at + NC * HALF]
+        )
+        block = jnp.concatenate([wide[:, q * piece : (q + 1) * piece] for q in range(NY)], axis=0)
+        out_ref[dest * local : (dest + 1) * local, width:] = block.astype(jnp.bfloat16)
+
+
+def project(slot, mine, rows, other, weight, stream):
+    count = slot.shape[0]
+    local = count // (NX * NZ)
     vmem = pl.BlockSpec(memory_space=pltpu.VMEM)
     return pl.pallas_call(
-        head_kernel,
-        out_shape=jax.ShapeDtypeStruct((NY, 128, width), jnp.float32),
-        in_specs=[
-            pl.BlockSpec(memory_space=pltpu.SMEM),
-            vmem,
-            vmem,
-            vmem,
-            pl.BlockSpec(memory_space=pl.ANY),
-        ],
-        out_specs=vmem,
-        scratch_shapes=[
-            pltpu.VMEM(weight.shape, jnp.bfloat16),
-            pltpu.VMEM((NY, NZ, HALF, 128), jnp.bfloat16),
-            pltpu.SemaphoreType.DMA((NX,)),
-        ],
+        project_kernel,
+        out_shape=(
+            jax.ShapeDtypeStruct((count, weight.shape[0] + HALF // NY), jnp.bfloat16),
+            jax.ShapeDtypeStruct((local, DC), jnp.bfloat16),
+        ),
+        in_specs=[vmem, pl.BlockSpec(memory_space=pltpu.SMEM), vmem, vmem, vmem, vmem],
+        out_specs=(vmem, vmem),
         compiler_params=pltpu.CompilerParams(vmem_limit_bytes=32 * 1024 * 1024),
-        name="head",
-    )(core, own, other, gain.reshape(NX * NZ * NC, HALF), weight)
+        name="project",
+    )(slot.reshape(1, count), mine, rows, other, weight, stream)
 
 
 def merge(peak, total, hit):
@@ -256,11 +375,12 @@
     latent = jnp.swapaxes(latent, 0, 1).reshape(own_rows, QL + DC)
     query_latent = row_norm(latent[:, :QL], query_gain)
     latent_part = row_norm(latent[:, QL : QL + DL], latent_gain)
-    rows = jnp.concatenate([query_latent, latent_part, latent[:, QL + DL :]], axis=1)
+    blank = jnp.zeros((own_rows, PAD), jnp.float32)
+    rows = jnp.concatenate([query_latent, latent_part, latent[:, QL + DL :], blank], axis=1)
     rows = rows.astype(jnp.bfloat16)
 
-    rows = share(rows, "z", NZ).reshape(NZ * own_rows, QL + DC)
-    rows = share(rows, ("x", "y"), NX * NY).reshape(row_count // NC, QL + DC)
+    rows = share(rows, "z", NZ).reshape(NZ * own_rows, -1)
+    rows = share(rows, ("x", "y"), NX * NY).reshape(row_count // NC, -1)
     other_rows = swap_cores(rows)
     place = jnp.arange(row_count // NC, dtype=jnp.int32)
     at_i = place % own_rows
@@ -274,60 +394,50 @@
     request_row = jnp.concatenate([row_ids(c), row_ids(1 - c)])
 
     weight = jnp.swapaxes(query_weight, 0, 1).reshape(slice_width * local_heads, QL)
-
-    def project(block):
-        part = lax.dot_general(
-            block[:, :QL], weight, (((1,), (1,)), ((), ())), preferred_element_type=jnp.float32
-        )
-        return part.astype(jnp.bfloat16)
-
-    query_part = jnp.concatenate([project(rows), project(other_rows)])
-    every_fresh = jnp.concatenate([rows[:, QL:], other_rows[:, QL:]])
     owner_row = (owner_place[:, None] * step_count + step_index[None, :]).reshape(row_count)
-    slot_of_place = jnp.zeros((row_count,), jnp.int32)
     row_index = jnp.arange(row_count, dtype=jnp.int32)
     same = request_row[None, :] == row_index[:, None]
     slot_of_place = jnp.sum(jnp.where(same, owner_row[:, None], 0), axis=0)
-    reorder = (slot_of_place[None, :] == row_index[:, None]).astype(jnp.bfloat16)
-    query_owned = jnp.dot(reorder, query_part, preferred_element_type=jnp.float32)
-    query_owned = query_owned.astype(jnp.bfloat16).reshape(dp_count, local_rows, -1)
-    own_reorder = (
-        slot_of_place[None, :] == (d * local_rows + jnp.arange(local_rows, dtype=jnp.int32))[:, None]
-    ).astype(jnp.bfloat16)
-    own_fresh = jnp.dot(own_reorder, every_fresh, preferred_element_type=jnp.float32)
-    own_fresh = own_fresh.astype(jnp.bfloat16).reshape(local_requests, step_count, DC)
 
     lane_rows = local_rows // NY
-    mine = hidden_state.reshape(dp_count, NC, HALF, NY, lane_rows)
-    mine = lax.dynamic_index_in_dim(mine, c, 1, keepdims=False)
-    mine = lax.dynamic_index_in_dim(mine, y, 2, keepdims=False)
-    mine = mine.reshape(dp_count, local_rows, HALF * lane_rows // local_rows)
     width = slice_width * local_heads
+    payload, own_fresh = project(
+        slot_of_place,
+        jnp.stack([d * local_rows, y, c]),
+        rows,
+        other_rows,
+        weight,
+        jnp.swapaxes(hidden_state, 0, 1),
+    )
+    own_fresh = own_fresh.reshape(local_requests, step_count, DC)
     arrived = lax.all_to_all(
-        jnp.concatenate([query_owned, mine], axis=2), DP, split_axis=0, concat_axis=0, tiled=True
-    )
-    stream_block = arrived[:, :, width:].reshape(dp_count, HALF, lane_rows)
-    stream_block = jnp.transpose(stream_block, (1, 0, 2)).reshape(HALF, dp_count * lane_rows)
-    arrived = arrived[:, :, :width].reshape(
-        dp_count, local_requests, step_count, slice_width, local_heads
-    )
-    queries = jnp.transpose(arrived, (1, 2, 4, 0, 3)).reshape(
-        local_requests, step_count * local_heads, DC
-    )
+        payload.reshape(dp_count, local_rows, -1), DP, split_axis=0, concat_axis=0, tiled=True
+    )
+    stream_block = arrived[:, :, width:].reshape(dp_count, NY, lane_rows, HALF // NY)
+    stream_block = jnp.transpose(stream_block, (1, 3, 0, 2)).reshape(HALF, dp_count * lane_rows)
+    packed = jnp.transpose(arrived[:, :, :width], (1, 2, 0))
 
     fresh_padded = jnp.pad(own_fresh, ((0, 0), (0, 16 - step_count), (0, 0)))
-    attended = attend(cache_length, queries, fresh_padded, latent_cache)
+    attended = attend(cache_length, packed, fresh_padded, latent_cache)
     attended = attended.reshape(local_requests, step_count, local_heads, DL)
     head_values = jnp.einsum(
         "ushc,hcv->ushv", attended, value_weight, preferred_element_type=jnp.float32
     )
     head_values = head_values.astype(jnp.bfloat16).reshape(local_rows, local_heads * value_width)
     head_values = share(head_values, "z", NZ).reshape(NZ * local_rows, -1)
-    head_values = share(head_values, "x", NX).reshape(row_count, -1)
+    head_values = jnp.concatenate(
+        [head_values]
+        + [
+            lax.ppermute(head_values, "x", [(i, (i + k) % NX) for i in range(NX)])
+            for k in range(1, NX)
+        ]
+    )
 
     turned = row_index.reshape(dp_count, NY, lane_rows).swapaxes(0, 1).reshape(row_count)
     turned_owner = owner_row.reshape(dp_count, NY, lane_rows).swapaxes(0, 1).reshape(row_count)
-    turn = (turned_owner[:, None] == row_index[None, :]).astype(jnp.bfloat16)
+    held = (x - row_index // (NZ * local_rows)) % NX * (NZ * local_rows)
+    held = held + row_index % (NZ * local_rows)
+    turn = (turned_owner[:, None] == held[None, :]).astype(jnp.bfloat16)
     head_values = jnp.dot(turn, head_values, preferred_element_type=jnp.float32)
     head_values = head_values.astype(jnp.bfloat16)
     terms = lax.dot_general(
@@ -342,12 +452,26 @@
     residual = (jnp.sum(kept, axis=0) + stream_block.astype(jnp.float32)).astype(jnp.bfloat16)
 
     residual = share(residual, "z", NZ)
-    residual = share(residual, ("x", "y"), NX * NY)
-    residual = residual.reshape(NX, NY, NZ, HALF, row_count // NY)
-    other = swap_cores(residual)
-    logits = head(c.reshape(1), residual, other, final_gain, head_weight)
-
+    squares = residual.astype(jnp.float32)
+    squares = jnp.sum(squares * squares, axis=(0, 1))
+    squares = squares + swap_cores(squares)
+    high = lax.reduce_precision(squares, 8, 7)
+    middle = lax.reduce_precision(squares - high, 8, 7)
+    parts = jnp.stack([high, middle, squares - high - middle])
+    parts = jnp.pad(parts, ((0, 16 - 3), (0, 0))).astype(jnp.bfloat16)
+    residual = residual.reshape(NZ * HALF, -1)
+    halves = jnp.concatenate([residual[: NZ // 2 * HALF], parts]), residual[NZ // 2 * HALF :]
+
+    def whole(parts):
+        return jnp.stack(parts[:3] + (jnp.concatenate(parts[3:]),))
+
+    pieces = ring(whole(ring(halves[0], "x")), "y") + ring(whole(ring(halves[1], "y")), "x")
+    place_of = jnp.stack([x, y, c])
     vocab_width = head_weight.shape[1]
+    head_weight = head_weight.reshape(NX, NZ, NC, HALF, vocab_width)
+    other = swap_cores(lax.dynamic_index_in_dim(head_weight, 1 - c, 2, keepdims=False))
+    logits = head(place_of, final_gain, head_weight, other, pieces)
+    logits = logits[0] + swap_cores(logits[1])
     logits = logits.reshape(row_count, vocab_width)
     vocab_start = (d * tp_count + t) * vocab_width
 

time: 297 us -> 267 us (0.90)
  blocking collectives: 126 us -> 69.4 us
  starting transfers between devices: 22 us -> 51.3 us
  waiting for transfers between devices: 66.1 us -> 80.7 us
  local copies, waits for them, and re-layouts: 28.9 us -> 19.1 us
  matrix products: 11.4 us -> 6.94 us
    all_to_all x5 -> x3, blocking collectives: 116 us -> 59.7 us  [share(): return lax.all_to_all(copies, axes, split_axis=0, concat_axis=0, tiled=True)]
    ppermute x0 -> x19, waiting for transfers between devices: none -> 34.3 us  [the longest x3 20.9 us: on_device(): lax.ppermute(head_values, 'x', [(i, (i + k) % NX) for i in range(NX)])]
    ppermute x0 -> x19, starting transfers between devices: none -> 27.4 us  [the longest x16 22.3 us: shift(): return lax.ppermute(block, axis, [(i, (i + step) % 4) for i in range(4)])]
    all_to_all x3, waiting for transfers between devices: 37.8 us -> 20.6 us  [share(): return lax.all_to_all(copies, axes, split_axis=0, concat_axis=0, tiled=True)]
    reshape x7 -> x3, local copies, waits for them, and re-layouts: 7.3 us -> 0.74 us  [the longest x2 0.72 us: head(): gain = jnp.transpose(gain.reshape(NX, NZ, NC, HALF), (0, 2, 1, 3))]
    dot_general x4 -> x0, matrix products: 4.45 us -> none  [the longest x2 3.11 us: project(): lax.dot_general(block[:, :QL], weight, (((1,), (1,)), ((), ())), preferre...]
    ppermute x4 -> x6, waiting for transfers between devices: 8.67 us -> 4.73 us  [swap_cores(): return lax.ppermute(block, 'c', [(0, 1), (1, 0)])]
    squeeze x0 -> x2, local copies, waits for them, and re-layouts: none -> 3.94 us  [the longest x1 2.86 us: on_device(): lax.dynamic_index_in_dim(head_weight, 1 - c, 2, keepdims=False)]
  transfers between devices with their start and end apart: 9 -> 30, of which waited for: 8 -> 17; matrix products, arithmetic and copies ran while one was open for 3% -> 5% of each run, Pallas kernels for 0% -> 0%
where the time goes in v2:
time: 267 us; the launch traced here: 266 us
  waiting for transfers between devices  80.7 us (30%)
  blocking collectives  69.4 us (26%)
  starting transfers between devices  51.3 us (19%)
  Pallas kernels  29.6 us (11%)
  local copies, waits for them, and re-layouts  19.1 us (7%)
  other arithmetic  8.11 us (3%)
  matrix products  6.94 us (3%)
    all_to_all x3, blocking collectives, share(): return lax.all_to_all(copies, axes, split_axis=0, concat_axis=0, tiled=True)  59.7 us
    ppermute x16, starting transfers between devices, shift(): return lax.ppermute(block, axis, [(i, (i + step) % 4) for i in range(4)])  22.3 us
    ppermute x3, waiting for transfers between devices, on_device(): lax.ppermute(head_values, 'x', [(i, (i + k) % NX) for i in range(NX)])  20.9 us
    all_to_all x3, waiting for transfers between devices, share(): return lax.all_to_all(copies, axes, split_axis=0, concat_axis=0, tiled=True)  20.6 us
    pallas_call x1, Pallas kernels, attend(): pl.pallas_call(attend_kernel, out_shape=jax.ShapeDtypeStruct((slots, rows...  18.9 us
    all_to_all x1, waiting for transfers between devices, on_device(): lax.all_to_all(payload.reshape(dp_count, local_rows, -1), DP, split_axis=...  15.5 us
    all_to_all x3, starting transfers between devices, share(): return lax.all_to_all(copies, axes, split_axis=0, concat_axis=0, tiled=True)  14.9 us
    ppermute x16, waiting for transfers between devices, shift(): return lax.ppermute(block, axis, [(i, (i + step) % 4) for i in range(4)])  13.3 us
  transfers between devices with their start and end apart: 30, of which 17 were waited for; matrix products, arithmetic and copies ran while one was open for 5% of the time, Pallas kernels for 0%

profile of v2, /device:TPU:32, one launch (start us, length us, event | category | flops | bytes accessed | tf_op | source)
XLA Modules:
  0.0 266.3 jit_solution(17678224525595419365)
XLA Ops:
  1.9 3.4 %convolution_multiply_fusion = f32[16,264]{1,0:T(8,128)S(1)} fusion(bf16[7168,264]{0,1:T(8,128)(2,1)} %param.17, bf16[7168,16]{0,1:T(8,128)(2,1)} %param.15, f32[7168]{0:T(1024)} %param.16, f32[16]{0:T(128)S(1)} %add_rsqrt_fusion.2), kind=kOutput, calls=%fused_computation.14 | convolution fusion | flops 60903552 | bytes 4059712 | tf_op jit(solution)/shard_map/dot_general | solution.py:367
  5.4 9.7 %all_to_all.45 = f32[8,2,264]{2,1,0:T(2,128)S(1)} all-to-all(f32[8,2,264]{2,1,0:T(2,128)S(1)} %reshape.306), channel_id=1, replica_groups=mesh['x'=4,'z'=8,'y'=4,'c'=2] {'y','c'}, dimensions={0} | all-to-all | bytes 33792 | tf_op jit(solution)/shard_map/all_to_all | solution.py:372
  15.8 15.3 %all_to_all.46 = bf16[8,2,2176]{2,1,0:T(2,128)(2,1)S(1)} all-to-all(bf16[8,2,2176]{2,1,0:T(2,128)(2,1)S(1)} %broadcast_in_dim.55), channel_id=1, replica_groups=mesh['x'=4,'z'=8,'y'=4,'c'=2] {'z'}, dimensions={0} | all-to-all | bytes 139264 | tf_op jit(solution)/shard_map/all_to_all | solution.py:33
  31.2 21.2 %all_to_all.47 = bf16[16,16,2176]{2,1,0:T(8,128)(2,1)S(1)} all-to-all(bf16[16,16,2176]{2,1,0:T(8,128)(2,1)S(1)} %broadcast_in_dim.60), channel_id=1, replica_groups=mesh['x'=4,'z'=8,'y'=4,'c'=2] {'x','y'}, dimensions={0} | all-to-all | bytes 2228224 | tf_op jit(solution)/shard_map/all_to_all | solution.py:33
  56.5 2.7 %project.1 = (bf16[512,316]{1,0:T(8,128)(2,1)S(1)}, bf16[16,576]{1,0:T(8,128)(2,1)S(1)}) custom-call(s32[1,512]{1,0:T(1,128)S(1)} %bitcast.160, s32[3]{0:T(128)S(1)} %add_add_fusion.1.mine_ref, bf16[256,2176]{1,0:T(8,128)(2,1)S(1)} %bitcast.155, bf16[256,2176]{1,0:T(8,128)(2,1)} %collective-permute-done.1.other_ref, bf16[288,1536]{1,0:T(8,128)(2,1)S(1)} %bitcast.158, ...), custom_call_target="tpu_custom_call" | custom-call | tf_op jit(solution)/shard_map/project/pallas_call | solution.py:317
  59.9 5.1 %all-to-all-start.3 = ((bf16[32,16,316]{2,1,0:T(8,128)(2,1)}), bf16[32,16,316]{2,1,0:T(8,128)(2,1)S(1)}, u32[]{:S(2)}, u32[]{:S(2)}) async-start(bf16[32,16,316]{2,1,0:T(8,128)(2,1)} %bitcast.159), calls=%async_computation.3 | async-start | bytes 786432 | tf_op jit(solution)/shard_map/all_to_all | solution.py:413
  65.1 15.5 %all-to-all-done.3 = bf16[32,16,316]{2,1,0:T(8,128)(2,1)S(1)} async-done(((bf16[32,16,316]{2,1,0:T(8,128)(2,1)}), bf16[32,16,316]{2,1,0:T(8,128)(2,1)S(1)}, u32[]{:S(2)}, u32[]{:S(2)}) %all-to-all-start.3) | async-done | bytes 323616 | tf_op jit(solution)/shard_map/all_to_all | solution.py:413
  81.4 1.6 copy.137
  83.0 18.9 %attend.1 = bf16[8,32,512]{2,1,0:T(8,128)(2,1)S(1)} custom-call(s32[8]{0:T(128)S(1)} %copy-done.5, bf16[16,288,32]{2,1,0:T(8,128)(2,1)S(1)} %bitcast.153, bf16[8,16,576]{2,1,0:T(8,128)(2,1)S(1)} %pad.9.fresh_ref, bf16[8,576,4096]{2,1,0:T(8,128)(2,1)} %bitcast.161), custom_call_target="tpu_custom_call" | custom-call | tf_op jit(solution)/shard_map/attend/pallas_call | solution.py:147
  102.6 23.2 %all_to_all.48 = bf16[8,16,2048]{2,1,0:T(8,128)(2,1)S(1)} all-to-all(bf16[8,16,2048]{2,1,0:T(8,128)(2,1)S(1)} %broadcast_in_dim.62), channel_id=1, replica_groups=mesh['x'=4,'z'=8,'y'=4,'c'=2] {'z'}, dimensions={0} | all-to-all | bytes 1048576 | tf_op jit(solution)/shard_map/all_to_all | solution.py:33
  125.7 2.8 %collective-permute-start.4 = (bf16[128,2048]{1,0:T(8,128)(2,1)S(1)}, bf16[128,2048]{1,0:T(8,128)(2,1)S(1)}, u32[]{:S(2)}, u32[]{:S(2)}) collective-permute-start(bf16[128,2048]{1,0:T(8,128)(2,1)S(1)} %bitcast.168), channel_id=1, source_target_pairs={{0,192},{64,0},{128,64},{192,128},{1,193},{65,1},{129,65},{193,129... | collective-permute-start | bytes 1572872 | tf_op jit(solution)/shard_map/ppermute | solution.py:431
  131.5 17.1 %collective-permute-done.4 = bf16[128,2048]{1,0:T(8,128)(2,1)S(1)} collective-permute-done((bf16[128,2048]{1,0:T(8,128)(2,1)S(1)}, bf16[128,2048]{1,0:T(8,128)(2,1)S(1)}, u32[]{:S(2)}, u32[]{:S(2)}) %collective-permute-start.4) | collective-permute-done | bytes 524320 | tf_op jit(solution)/shard_map/ppermute | solution.py:431
  148.7 3.8 %collective-permute-done.2 = bf16[128,2048]{1,0:T(8,128)(2,1)} collective-permute-done((bf16[128,2048]{1,0:T(8,128)(2,1)S(1)}, bf16[128,2048]{1,0:T(8,128)(2,1)}, u32[]{:S(2)}, u32[]{:S(2)}) %collective-permute-start.2) | collective-permute-done | bytes 524320 | tf_op jit(solution)/shard_map/ppermute | solution.py:431
  152.5 3.1 %fusion.10 = f32[512,224]{0,1:T(8,128)S(1)} fusion(bf16[224,2048]{1,0:T(8,128)(2,1)S(1)} %copy-done.19, bf16[128,2048]{1,0:T(8,128)(2,1)S(1)} %collective-permute-done.4, bf16[128,2048]{1,0:T(8,128)(2,1)} %collective-permute-done.3, bf16[128,2048]{1,0:T(8,128)(2,1)} %collective-permute-done.2, bf16[128,2048]{1,0:T(8,128)(2,1)S(1)} %bitcast.171, ...), kind=kOutput, calls=%fused_computation.11 | convolution fusion | flops 1553203200 | bytes 3477504 | tf_op jit(solution)/shard_map/dot_general | solution.py:443
  158.0 3.4 %all-to-all-start.5 = ((f32[4,112,128]{2,1,0:T(8,128)}), f32[4,112,128]{2,1,0:T(8,128)S(1)}, u32[]{:S(2)}, u32[]{:S(2)}) async-start(f32[4,112,128]{2,1,0:T(8,128)} %copy.116), calls=%async_computation.5 | async-start | bytes 458752 | tf_op jit(solution)/shard_map/all_to_all | solution.py:451
  162.7 5.5 %all-to-all-done.5 = f32[4,112,128]{2,1,0:T(8,128)S(1)} async-done(((f32[4,112,128]{2,1,0:T(8,128)}), f32[4,112,128]{2,1,0:T(8,128)S(1)}, u32[]{:S(2)}, u32[]{:S(2)}) %all-to-all-start.5) | async-done | bytes 229408 | tf_op jit(solution)/shard_map/all_to_all | solution.py:451
  169.0 5.0 %all-to-all-start.6 = ((bf16[8,112,128]{2,1,0:T(8,128)(2,1)}), bf16[8,112,128]{2,1,0:T(8,128)(2,1)S(1)}, u32[]{:S(2)}, u32[]{:S(2)}) async-start(bf16[8,112,128]{2,1,0:T(8,128)(2,1)} %broadcast_in_dim.63), calls=%async_computation.6 | async-start | bytes 458752 | tf_op jit(solution)/shard_map/all_to_all | solution.py:33
  174.0 2.9 %dynamic-slice_bitcast_fusion = bf16[4,8,112,256]{3,2,1,0:T(8,128)(2,1)} fusion(bf16[4,8,2,112,256]{4,3,2,1,0:T(8,128)(2,1)} %bitcast.162, s32[]{:T(128)S(6)} %select_n.101), kind=kLoop, calls=%fused_computation.10 | loop fusion | bytes 3670020 | tf_op jit(solution)/shard_map/jit(dynamic_index_in_dim)/squeeze | solution.py:472
  176.9 6.3 %all-to-all-done.6 = bf16[8,112,128]{2,1,0:T(8,128)(2,1)S(1)} async-done(((bf16[8,112,128]{2,1,0:T(8,128)(2,1)}), bf16[8,112,128]{2,1,0:T(8,128)(2,1)S(1)}, u32[]{:S(2)}, u32[]{:S(2)}) %all-to-all-start.6) | async-done | bytes 229408 | tf_op jit(solution)/shard_map/all_to_all | solution.py:33
  189.1 2.4 collective-permute-start.18
  193.8 3.1 %collective-permute-done.17 = bf16[224,128]{1,0:T(8,128)(2,1)S(1)} collective-permute-done((bf16[224,128]{1,0:T(8,128)(2,1)S(1)}, bf16[224,128]{1,0:T(8,128)(2,1)S(1)}, u32[]{:S(2)}, u32[]{:S(2)}) %collective-permute-start.17) | collective-permute-done | bytes 57376 | tf_op jit(solution)/shard_map/ppermute | solution.py:41
  199.0 2.7 %collective-permute-start.12 = (bf16[4,464,128]{2,1,0:T(8,128)(2,1)S(1)}, bf16[4,464,128]{2,1,0:T(8,128)(2,1)S(1)}, u32[]{:S(2)}, u32[]{:S(2)}) collective-permute-start(bf16[4,464,128]{2,1,0:T(8,128)(2,1)S(1)} %pad_maximum_fusion.rest_0_), channel_id=1, source_target_pairs={{0,6},{2,0},{4,2},{6,4},{1,7},{3,1},{5,3},{7,5},{8,14},{10,8},{12,... | collective-permute-start | bytes 1425416 | tf_op jit(solution)/shard_map/ppermute | solution.py:41
  201.9 3.2 %collective-permute-start.20 = (bf16[4,448,128]{2,1,0:T(8,128)(2,1)S(1)}, bf16[4,448,128]{2,1,0:T(8,128)(2,1)S(1)}, u32[]{:S(2)}, u32[]{:S(2)}) collective-permute-start(bf16[4,448,128]{2,1,0:T(8,128)(2,1)S(1)} %pad_maximum_fusion.1.rest_5_), channel_id=1, source_target_pairs={{0,192},{64,0},{128,64},{192,128},{1,193},{65,1},{129,65},{193,129... | collective-permute-start | bytes 1376264 | tf_op jit(solution)/shard_map/ppermute | solution.py:41
  205.1 5.0 %collective-permute-done.11.rest_1_ = bf16[4,464,128]{2,1,0:T(8,128)(2,1)S(1)} collective-permute-done((bf16[4,464,128]{2,1,0:T(8,128)(2,1)S(1)}, bf16[4,464,128]{2,1,0:T(8,128)(2,1)S(1)}, u32[]{:S(2)}, u32[]{:S(2)}) %collective-permute-start.11) | collective-permute-done | bytes 475168 | tf_op jit(solution)/shard_map/ppermute | solution.py:41
  210.2 3.5 %collective-permute-start.14 = (bf16[2,464,128]{2,1,0:T(8,128)(2,1)S(1)}, bf16[2,464,128]{2,1,0:T(8,128)(2,1)}, u32[]{:S(2)}, u32[]{:S(2)}) collective-permute-start(bf16[2,464,128]{2,1,0:T(8,128)(2,1)S(1)} %slice.122), channel_id=1, source_target_pairs={{0,6},{2,0},{4,2},{6,4},{1,7},{3,1},{5,3},{7,5},{8,14},{10,8},{12,... | collective-permute-start | bytes 712712 | tf_op jit(solution)/shard_map/ppermute | solution.py:41
  215.5 3.0 %collective-permute-start.22 = (bf16[2,448,128]{2,1,0:T(8,128)(2,1)}, bf16[2,448,128]{2,1,0:T(8,128)(2,1)}, u32[]{:S(2)}, u32[]{:S(2)}) collective-permute-start(bf16[2,448,128]{2,1,0:T(8,128)(2,1)} %slice.127), channel_id=1, source_target_pairs={{0,192},{64,0},{128,64},{192,128},{1,193},{65,1},{129,65},{193,129... | collective-permute-start | bytes 688136 | tf_op jit(solution)/shard_map/ppermute | solution.py:41
  219.9 2.2 collective-permute-done.21.rest_8_
  222.4 8.0 %head.1 = f32[2,4,128,256]{3,2,1,0:T(8,128)} custom-call(s32[3]{0:T(128)} %add_add_fusion.place_ref, f32[4,2,8,112]{3,2,1,0:T(8,128)} %bitcast.185, bf16[4,8,2,112,256]{4,3,2,1,0:T(8,128)(2,1)} %bitcast.163, bf16[4,8,112,256]{3,2,1,0:T(8,128)(2,1)} %collective-permute-done.other_hbm, bf16[4,464,128]{2,1,0:T(8,128)(2,1)} %copy-done.7, ...), custom_call_target="tpu_custom_call" | custom-call | tf_op jit(solution)/shard_map/head/pallas_call | solution.py:254
  237.0 3.3 %all-to-all-start.7 = ((f32[4,3,4,128]{3,2,1,0:T(4,128)}), f32[4,3,4,128]{3,2,1,0:T(4,128)S(1)}, u32[]{:S(2)}, u32[]{:S(2)}) async-start(f32[4,3,4,128]{3,2,1,0:T(4,128)} %broadcast_in_dim.64), calls=%async_computation.7 | async-start | bytes 49152 | tf_op jit(solution)/shard_map/all_to_all | solution.py:33
  240.8 4.9 %all-to-all-done.7 = f32[4,3,4,128]{3,2,1,0:T(4,128)S(1)} async-done(((f32[4,3,4,128]{3,2,1,0:T(4,128)}), f32[4,3,4,128]{3,2,1,0:T(4,128)S(1)}, u32[]{:S(2)}, u32[]{:S(2)}) %all-to-all-start.7) | async-done | bytes 24608 | tf_op jit(solution)/shard_map/all_to_all | solution.py:33
  246.4 6.6 %all-to-all-start.8 = ((f32[32,3,4,128]{3,2,1,0:T(4,128)}), f32[32,3,4,128]{3,2,1,0:T(4,128)S(1)}, u32[]{:S(2)}, u32[]{:S(2)}) async-start(f32[32,3,4,128]{3,2,1,0:T(4,128)} %broadcast_in_dim.68), calls=%async_computation.8 | async-start | bytes 393216 | tf_op jit(solution)/shard_map/all_to_all | solution.py:33
  254.0 9.4 %all-to-all-done.8 = f32[32,3,4,128]{3,2,1,0:T(4,128)S(1)} async-done(((f32[32,3,4,128]{3,2,1,0:T(4,128)}), f32[32,3,4,128]{3,2,1,0:T(4,128)S(1)}, u32[]{:S(2)}, u32[]{:S(2)}) %all-to-all-start.8) | async-done | bytes 196640 | tf_op jit(solution)/shard_map/all_to_all | solution.py:33
  (193 shorter events, 41.2 us)
Async XLA Ops:
  0.6 101.4 %copy-start = (bf16[16,512,128]{2,1,0:T(8,128)(2,1)S(1)}, bf16[16,512,128]{2,1,0:T(8,128)(2,1)}, u32[]{:S(2)}) copy-start(bf16[16,512,128]{2,1,0:T(8,128)(2,1)} %param.25) | copy-start | bytes 6291460
  52.4 2.9 %collective-permute-start.1 = (bf16[256,2176]{1,0:T(8,128)(2,1)S(1)}, bf16[256,2176]{1,0:T(8,128)(2,1)}, u32[]{:S(2)}, u32[]{:S(2)}) collective-permute-start(bf16[256,2176]{1,0:T(8,128)(2,1)S(1)} %bitcast.154), channel_id=1, source_target_pairs={{0,1},{1,0},{2,3},{3,2},{4,5},{5,4},{6,7},{7,6},{8,9},{9,8},{10,11... | collective-permute-start | bytes 3342344 | tf_op jit(solution)/shard_map/ppermute | solution.py:37
  59.9 20.7 %all-to-all-start.3 = ((bf16[32,16,316]{2,1,0:T(8,128)(2,1)}), bf16[32,16,316]{2,1,0:T(8,128)(2,1)S(1)}, u32[]{:S(2)}, u32[]{:S(2)}) async-start(bf16[32,16,316]{2,1,0:T(8,128)(2,1)} %bitcast.159), calls=%async_computation.3 | async-start | bytes 786432 | tf_op jit(solution)/shard_map/all_to_all | solution.py:413
  102.0 50.5 %copy-start.19 = (bf16[224,2048]{1,0:T(8,128)(2,1)S(1)}, bf16[224,2048]{1,0:T(8,128)(2,1)}, u32[]{:S(2)}) copy-start(bf16[224,2048]{1,0:T(8,128)(2,1)} %param.26) | copy-start | bytes 2752516
  125.7 22.9 %collective-permute-start.4 = (bf16[128,2048]{1,0:T(8,128)(2,1)S(1)}, bf16[128,2048]{1,0:T(8,128)(2,1)S(1)}, u32[]{:S(2)}, u32[]{:S(2)}) collective-permute-start(bf16[128,2048]{1,0:T(8,128)(2,1)S(1)} %bitcast.168), channel_id=1, source_target_pairs={{0,192},{64,0},{128,64},{192,128},{1,193},{65,1},{129,65},{193,129... | collective-permute-start | bytes 1572872 | tf_op jit(solution)/shard_map/ppermute | solution.py:431
  128.5 20.1 %collective-permute-start.3 = (bf16[128,2048]{1,0:T(8,128)(2,1)S(1)}, bf16[128,2048]{1,0:T(8,128)(2,1)}, u32[]{:S(2)}, u32[]{:S(2)}) collective-permute-start(bf16[128,2048]{1,0:T(8,128)(2,1)S(1)} %bitcast.169), channel_id=1, source_target_pairs={{0,128},{64,192},{128,0},{192,64},{1,129},{65,193},{129,1},{193,65... | collective-permute-start | bytes 1572872 | tf_op jit(solution)/shard_map/ppermute | solution.py:431
  130.1 22.4 %collective-permute-start.2 = (bf16[128,2048]{1,0:T(8,128)(2,1)S(1)}, bf16[128,2048]{1,0:T(8,128)(2,1)}, u32[]{:S(2)}, u32[]{:S(2)}) collective-permute-start(bf16[128,2048]{1,0:T(8,128)(2,1)S(1)} %bitcast.170), channel_id=1, source_target_pairs={{0,64},{64,128},{128,192},{192,0},{1,65},{65,129},{129,193},{193,1... | collective-permute-start | bytes 1572872 | tf_op jit(solution)/shard_map/ppermute | solution.py:431
  155.6 1.6 collective-permute-start.5
  158.0 10.3 %all-to-all-start.5 = ((f32[4,112,128]{2,1,0:T(8,128)}), f32[4,112,128]{2,1,0:T(8,128)S(1)}, u32[]{:S(2)}, u32[]{:S(2)}) async-start(f32[4,112,128]{2,1,0:T(8,128)} %copy.116), calls=%async_computation.5 | async-start | bytes 458752 | tf_op jit(solution)/shard_map/all_to_all | solution.py:451
  169.0 14.2 %all-to-all-start.6 = ((bf16[8,112,128]{2,1,0:T(8,128)(2,1)}), bf16[8,112,128]{2,1,0:T(8,128)(2,1)S(1)}, u32[]{:S(2)}, u32[]{:S(2)}) async-start(bf16[8,112,128]{2,1,0:T(8,128)(2,1)} %broadcast_in_dim.63), calls=%async_computation.6 | async-start | bytes 458752 | tf_op jit(solution)/shard_map/all_to_all | solution.py:33
  176.9 43.0 %collective-permute-start = (bf16[4,8,112,256]{3,2,1,0:T(8,128)(2,1)}, bf16[4,8,112,256]{3,2,1,0:T(8,128)(2,1)}, u32[]{:S(2)}, u32[]{:S(2)}) collective-permute-start(bf16[4,8,112,256]{3,2,1,0:T(8,128)(2,1)} %dynamic-slice_bitcast_fusion), channel_id=1, source_target_pairs={{0,1},{1,0},{2,3},{3,2},{4,5},{5,4},{6,7},{7,6},{8,9},{9,8},{10,11... | collective-permute-start | bytes 5505032 | tf_op jit(solution)/shard_map/ppermute | solution.py:37
  183.3 2.2 collective-permute-start.6
  183.5 5.6 %collective-permute-start.16 = (bf16[448,128]{1,0:T(8,128)(2,1)S(1)}, bf16[448,128]{1,0:T(8,128)(2,1)S(1)}, u32[]{:S(2)}, u32[]{:S(2)}) collective-permute-start(bf16[448,128]{1,0:T(8,128)(2,1)S(1)} %bitcast.172), channel_id=1, source_target_pairs={{0,6},{2,0},{4,2},{6,4},{1,7},{3,1},{5,3},{7,5},{8,14},{10,8},{12,... | collective-permute-start | bytes 344072 | tf_op jit(solution)/shard_map/ppermute | solution.py:41
  184.7 6.8 %collective-permute-start.15 = (bf16[448,128]{1,0:T(8,128)(2,1)S(1)}, bf16[448,128]{1,0:T(8,128)(2,1)S(1)}, u32[]{:S(2)}, u32[]{:S(2)}) collective-permute-start(bf16[448,128]{1,0:T(8,128)(2,1)S(1)} %bitcast.173), channel_id=1, source_target_pairs={{0,2},{2,4},{4,6},{6,0},{1,3},{3,5},{5,7},{7,1},{8,10},{10,12},{12... | collective-permute-start | bytes 344072 | tf_op jit(solution)/shard_map/ppermute | solution.py:41
  185.6 5.9 %collective-permute-start.8 = (bf16[464,128]{1,0:T(8,128)(2,1)S(1)}, bf16[464,128]{1,0:T(8,128)(2,1)S(1)}, u32[]{:S(2)}, u32[]{:S(2)}) collective-permute-start(bf16[464,128]{1,0:T(8,128)(2,1)S(1)} %get-tuple-element.16), channel_id=1, source_target_pairs={{0,192},{64,0},{128,64},{192,128},{1,193},{65,1},{129,65},{193,129... | collective-permute-start | bytes 356360 | tf_op jit(solution)/shard_map/ppermute | solution.py:41
  186.5 6.3 %collective-permute-start.7 = (bf16[464,128]{1,0:T(8,128)(2,1)S(1)}, bf16[464,128]{1,0:T(8,128)(2,1)S(1)}, u32[]{:S(2)}, u32[]{:S(2)}) collective-permute-start(bf16[464,128]{1,0:T(8,128)(2,1)S(1)} %get-tuple-element.16), channel_id=1, source_target_pairs={{0,64},{64,128},{128,192},{192,0},{1,65},{65,129},{129,193},{193,1... | collective-permute-start | bytes 356360 | tf_op jit(solution)/shard_map/ppermute | solution.py:41
  189.1 4.7 %collective-permute-start.18 = (bf16[224,128]{1,0:T(8,128)(2,1)S(1)}, bf16[224,128]{1,0:T(8,128)(2,1)S(1)}, u32[]{:S(2)}, u32[]{:S(2)}) collective-permute-start(bf16[224,128]{1,0:T(8,128)(2,1)S(1)} %slice.125), channel_id=1, source_target_pairs={{0,6},{2,0},{4,2},{6,4},{1,7},{3,1},{5,3},{7,5},{8,14},{10,8},{12,... | collective-permute-start | bytes 172040 | tf_op jit(solution)/shard_map/ppermute | solution.py:41
  191.5 5.5 %collective-permute-start.17 = (bf16[224,128]{1,0:T(8,128)(2,1)S(1)}, bf16[224,128]{1,0:T(8,128)(2,1)S(1)}, u32[]{:S(2)}, u32[]{:S(2)}) collective-permute-start(bf16[224,128]{1,0:T(8,128)(2,1)S(1)} %slice.124), channel_id=1, source_target_pairs={{0,2},{2,4},{4,6},{6,0},{1,3},{3,5},{5,7},{7,1},{8,10},{10,12},{12... | collective-permute-start | bytes 172040 | tf_op jit(solution)/shard_map/ppermute | solution.py:41
  191.6 5.4 %collective-permute-start.10 = (bf16[232,128]{1,0:T(8,128)(2,1)S(1)}, bf16[232,128]{1,0:T(8,128)(2,1)S(1)}, u32[]{:S(2)}, u32[]{:S(2)}) collective-permute-start(bf16[232,128]{1,0:T(8,128)(2,1)S(1)} %slice.120), channel_id=1, source_target_pairs={{0,192},{64,0},{128,64},{192,128},{1,193},{65,1},{129,65},{193,129... | collective-permute-start | bytes 178184 | tf_op jit(solution)/shard_map/ppermute | solution.py:41
  192.8 5.5 %collective-permute-start.9 = (bf16[232,128]{1,0:T(8,128)(2,1)S(1)}, bf16[232,128]{1,0:T(8,128)(2,1)S(1)}, u32[]{:S(2)}, u32[]{:S(2)}) collective-permute-start(bf16[232,128]{1,0:T(8,128)(2,1)S(1)} %slice.119), channel_id=1, source_target_pairs={{0,64},{64,128},{128,192},{192,0},{1,65},{65,129},{129,193},{193,1... | collective-permute-start | bytes 178184 | tf_op jit(solution)/shard_map/ppermute | solution.py:41
  198.4 11.7 %collective-permute-start.11 = (bf16[4,464,128]{2,1,0:T(8,128)(2,1)S(1)}, bf16[4,464,128]{2,1,0:T(8,128)(2,1)S(1)}, u32[]{:S(2)}, u32[]{:S(2)}) collective-permute-start(bf16[4,464,128]{2,1,0:T(8,128)(2,1)S(1)} %pad_maximum_fusion.rest_0_), channel_id=1, source_target_pairs={{0,2},{2,4},{4,6},{6,0},{1,3},{3,5},{5,7},{7,1},{8,10},{10,12},{12... | collective-permute-start | bytes 1425416 | tf_op jit(solution)/shard_map/ppermute | solution.py:41
  199.0 11.2 %collective-permute-start.12 = (bf16[4,464,128]{2,1,0:T(8,128)(2,1)S(1)}, bf16[4,464,128]{2,1,0:T(8,128)(2,1)S(1)}, u32[]{:S(2)}, u32[]{:S(2)}) collective-permute-start(bf16[4,464,128]{2,1,0:T(8,128)(2,1)S(1)} %pad_maximum_fusion.rest_0_), channel_id=1, source_target_pairs={{0,6},{2,0},{4,2},{6,4},{1,7},{3,1},{5,3},{7,5},{8,14},{10,8},{12,... | collective-permute-start | bytes 1425416 | tf_op jit(solution)/shard_map/ppermute | solution.py:41
  201.8 12.0 %collective-permute-start.19 = (bf16[4,448,128]{2,1,0:T(8,128)(2,1)S(1)}, bf16[4,448,128]{2,1,0:T(8,128)(2,1)S(1)}, u32[]{:S(2)}, u32[]{:S(2)}) collective-permute-start(bf16[4,448,128]{2,1,0:T(8,128)(2,1)S(1)} %pad_maximum_fusion.1.rest_5_), channel_id=1, source_target_pairs={{0,64},{64,128},{128,192},{192,0},{1,65},{65,129},{129,193},{193,1... | collective-permute-start | bytes 1376264 | tf_op jit(solution)/shard_map/ppermute | solution.py:41
  201.9 12.9 %collective-permute-start.20 = (bf16[4,448,128]{2,1,0:T(8,128)(2,1)S(1)}, bf16[4,448,128]{2,1,0:T(8,128)(2,1)S(1)}, u32[]{:S(2)}, u32[]{:S(2)}) collective-permute-start(bf16[4,448,128]{2,1,0:T(8,128)(2,1)S(1)} %pad_maximum_fusion.1.rest_5_), channel_id=1, source_target_pairs={{0,192},{64,0},{128,64},{192,128},{1,193},{65,1},{129,65},{193,129... | collective-permute-start | bytes 1376264 | tf_op jit(solution)/shard_map/ppermute | solution.py:41
  210.1 12.3 %collective-permute-start.13 = (bf16[2,464,128]{2,1,0:T(8,128)(2,1)S(1)}, bf16[2,464,128]{2,1,0:T(8,128)(2,1)}, u32[]{:S(2)}, u32[]{:S(2)}) collective-permute-start(bf16[2,464,128]{2,1,0:T(8,128)(2,1)S(1)} %slice.121), channel_id=1, source_target_pairs={{0,2},{2,4},{4,6},{6,0},{1,3},{3,5},{5,7},{7,1},{8,10},{10,12},{12... | collective-permute-start | bytes 712712 | tf_op jit(solution)/shard_map/ppermute | solution.py:41
  210.2 12.1 %collective-permute-start.14 = (bf16[2,464,128]{2,1,0:T(8,128)(2,1)S(1)}, bf16[2,464,128]{2,1,0:T(8,128)(2,1)}, u32[]{:S(2)}, u32[]{:S(2)}) collective-permute-start(bf16[2,464,128]{2,1,0:T(8,128)(2,1)S(1)} %slice.122), channel_id=1, source_target_pairs={{0,6},{2,0},{4,2},{6,4},{1,7},{3,1},{5,3},{7,5},{8,14},{10,8},{12,... | collective-permute-start | bytes 712712 | tf_op jit(solution)/shard_map/ppermute | solution.py:41
  214.5 7.5 %collective-permute-start.21 = (bf16[2,448,128]{2,1,0:T(8,128)(2,1)}, bf16[2,448,128]{2,1,0:T(8,128)(2,1)}, u32[]{:S(2)}, u32[]{:S(2)}) collective-permute-start(bf16[2,448,128]{2,1,0:T(8,128)(2,1)} %slice.126), channel_id=1, source_target_pairs={{0,64},{64,128},{128,192},{192,0},{1,65},{65,129},{129,193},{193,1... | collective-permute-start | bytes 688136 | tf_op jit(solution)/shard_map/ppermute | solution.py:41
  215.5 6.9 %collective-permute-start.22 = (bf16[2,448,128]{2,1,0:T(8,128)(2,1)}, bf16[2,448,128]{2,1,0:T(8,128)(2,1)}, u32[]{:S(2)}, u32[]{:S(2)}) collective-permute-start(bf16[2,448,128]{2,1,0:T(8,128)(2,1)} %slice.127), channel_id=1, source_target_pairs={{0,192},{64,0},{128,64},{192,128},{1,193},{65,1},{129,65},{193,129... | collective-permute-start | bytes 688136 | tf_op jit(solution)/shard_map/ppermute | solution.py:41
  231.5 2.0 collective-permute-start.23
  235.1 1.3 collective-permute-start.24
  237.0 8.6 %all-to-all-start.7 = ((f32[4,3,4,128]{3,2,1,0:T(4,128)}), f32[4,3,4,128]{3,2,1,0:T(4,128)S(1)}, u32[]{:S(2)}, u32[]{:S(2)}) async-start(f32[4,3,4,128]{3,2,1,0:T(4,128)} %broadcast_in_dim.64), calls=%async_computation.7 | async-start | bytes 49152 | tf_op jit(solution)/shard_map/all_to_all | solution.py:33
  246.4 16.9 %all-to-all-start.8 = ((f32[32,3,4,128]{3,2,1,0:T(4,128)}), f32[32,3,4,128]{3,2,1,0:T(4,128)S(1)}, u32[]{:S(2)}, u32[]{:S(2)}) async-start(f32[32,3,4,128]{3,2,1,0:T(4,128)} %broadcast_in_dim.68), calls=%async_computation.8 | async-start | bytes 393216 | tf_op jit(solution)/shard_map/all_to_all | solution.py:33
  (18 other events, 283.0 us)

commit v3 on v2

--- a/solution.py
+++ b/solution.py
@@ -94,47 +94,46 @@
         step_at = lax.broadcasted_iota(jnp.int32, new.shape, 0) // (rows // 2)
         new = jnp.where(key_at <= step_at, new, masked_score)
 
-        def score(chunk, peak):
-            copy(slot, chunk).wait()
-            s = jnp.dot(q, kbuf[slot, chunk], preferred_element_type=jnp.float32) * score_scale
-            at = chunk * CHUNK + lax.broadcasted_iota(jnp.int32, s.shape, 1)
-            s = jnp.where(at < length, s, masked_score)
-            sbuf[chunk] = s
-            for lane in range(0, CHUNK, 128):
-                peak = jnp.maximum(peak, s[:, lane : lane + 128])
-            return peak
-
-        peak = lax.fori_loop(0, live, score, jnp.full((rows, 128), masked_score, jnp.float32))
-        peak = jnp.maximum(
-            jnp.max(peak, axis=-1, keepdims=True), jnp.max(new, axis=-1, keepdims=True)
-        )
-        new = jnp.exp(new - peak)
-
-        def lift(chunk, total):
-            e = jnp.exp(sbuf[chunk] - peak)
-            sbuf[chunk] = e
-            for lane in range(0, CHUNK, 128):
-                total = total + e[:, lane : lane + 128]
-            return total
-
-        total = lax.fori_loop(0, live, lift, jnp.zeros((rows, 128), jnp.float32))
-        total = jnp.sum(total, axis=-1, keepdims=True) + jnp.sum(new, axis=-1, keepdims=True)
-        inverse = 1.0 / total
-        mixed = jnp.dot(
-            (new * inverse).astype(jnp.bfloat16), fresh[:, :DL], preferred_element_type=jnp.float32
-        )
-
-        def mix(chunk, acc):
-            weight = (sbuf[chunk] * inverse).astype(jnp.bfloat16)
-            return acc + lax.dot_general(
-                weight,
-                kbuf[slot, chunk, :DL, :],
-                (((1,), (1,)), ((), ())),
+        def straight(count):
+            peak = jnp.max(new, axis=-1, keepdims=True)
+            wide = jnp.full((rows, 128), masked_score, jnp.float32)
+            for chunk in range(count):
+                copy(slot, chunk).wait()
+                s = jnp.dot(q, kbuf[slot, chunk], preferred_element_type=jnp.float32) * score_scale
+                if chunk == count - 1:
+                    at = chunk * CHUNK + lax.broadcasted_iota(jnp.int32, s.shape, 1)
+                    s = jnp.where(at < length, s, masked_score)
+                sbuf[chunk] = s
+                for lane in range(0, CHUNK, 128):
+                    wide = jnp.maximum(wide, s[:, lane : lane + 128])
+            peak = jnp.maximum(peak, jnp.max(wide, axis=-1, keepdims=True))
+            lifted = jnp.exp(new - peak)
+            wide = jnp.zeros((rows, 128), jnp.float32)
+            for chunk in range(count):
+                e = jnp.exp(sbuf[chunk] - peak)
+                sbuf[chunk] = e
+                for lane in range(0, CHUNK, 128):
+                    wide = wide + e[:, lane : lane + 128]
+            total = jnp.sum(wide, axis=-1, keepdims=True)
+            total = total + jnp.sum(lifted, axis=-1, keepdims=True)
+            inverse = 1.0 / total
+            mixed = jnp.dot(
+                (lifted * inverse).astype(jnp.bfloat16),
+                fresh[:, :DL],
                 preferred_element_type=jnp.float32,
             )
-
-        mixed = lax.fori_loop(0, live, mix, mixed)
-        out_ref[slot] = mixed.astype(jnp.bfloat16)
+            for chunk in range(count):
+                weight = (sbuf[chunk] * inverse).astype(jnp.bfloat16)
+                mixed = mixed + lax.dot_general(
+                    weight,
+                    kbuf[slot, chunk, :DL, :],
+                    (((1,), (1,)), ((), ())),
+                    preferred_element_type=jnp.float32,
+                )
+            out_ref[slot] = mixed.astype(jnp.bfloat16)
+
+        for count in range(1, chunks + 1):
+            pl.when(live == count)(lambda count=count: straight(count))
         return carry
 
     lax.fori_loop(0, slots, one_slot, 0)
@@ -270,19 +269,28 @@
 
 
 def project_kernel(
-    slot_ref, mine_ref, rows_ref, other_ref, weight_ref, stream_ref, out_ref, fresh_ref
+    owner_ref, mine_ref, rows_ref, other_ref, weight_ref, stream_ref, out_ref, fresh_ref
 ):
-    count = slot_ref.shape[1]
-    half = count // NC
+    half = rows_ref.shape[0]
+    count = half * NC
     width = weight_ref.shape[0]
     total = None
     fresh = None
+    requests = owner_ref.shape[1]
+    owner = jnp.broadcast_to(owner_ref[...].astype(jnp.float32), (8, requests))
+    owner = owner.astype(jnp.bfloat16)
+    place = lax.broadcasted_iota(jnp.int32, (1, half), 1)
+    base = ((place >> 6) * NZ + ((place >> 1) & (NZ - 1))) * (NY * NC) + ((place >> 4) & 3) * NC
     for part, ref in enumerate((rows_ref, other_ref)):
         term = lax.dot_general(
             ref[:, :QL], weight_ref[...], (((1,), (1,)), ((), ())),
             preferred_element_type=jnp.float32,
         ).astype(jnp.bfloat16)
-        slot = slot_ref[:, part * half : (part + 1) * half]
+        core = mine_ref[2] if part == 0 else 1 - mine_ref[2]
+        holds = lax.broadcasted_iota(jnp.int32, (requests, half), 0) == base + core
+        holds = jnp.where(holds, 1.0, 0.0).astype(jnp.bfloat16)
+        slot = jnp.dot(owner, holds, preferred_element_type=jnp.float32)[:1]
+        slot = slot.astype(jnp.int32) * 2 + (place & 1)
         wanted = lax.broadcasted_iota(jnp.int32, (count, half), 0)
         pick = jnp.where(slot == wanted, 1.0, 0.0).astype(jnp.bfloat16)
         term = jnp.dot(pick, term, preferred_element_type=jnp.float32)
@@ -310,8 +318,8 @@
         out_ref[dest * local : (dest + 1) * local, width:] = block.astype(jnp.bfloat16)
 
 
-def project(slot, mine, rows, other, weight, stream):
-    count = slot.shape[0]
+def project(owner, mine, rows, other, weight, stream):
+    count = rows.shape[0] * NC
     local = count // (NX * NZ)
     vmem = pl.BlockSpec(memory_space=pltpu.VMEM)
     return pl.pallas_call(
@@ -324,7 +332,7 @@
         out_specs=(vmem, vmem),
         compiler_params=pltpu.CompilerParams(vmem_limit_bytes=32 * 1024 * 1024),
         name="project",
-    )(slot.reshape(1, count), mine, rows, other, weight, stream)
+    )(owner.reshape(1, -1), mine, rows, other, weight, stream)
 
 
 def merge(peak, total, hit):
@@ -382,27 +390,14 @@
     rows = share(rows, "z", NZ).reshape(NZ * own_rows, -1)
     rows = share(rows, ("x", "y"), NX * NY).reshape(row_count // NC, -1)
     other_rows = swap_cores(rows)
-    place = jnp.arange(row_count // NC, dtype=jnp.int32)
-    at_i = place % own_rows
-    at_z = place // own_rows % NZ
-    at_y = place // (own_rows * NZ) % NY
-    at_x = place // (own_rows * NZ * NY)
-
-    def row_ids(core):
-        return ((at_x * NZ + at_z) * tp_count + at_y * NC + core) * own_rows + at_i
-
-    request_row = jnp.concatenate([row_ids(c), row_ids(1 - c)])
-
     weight = jnp.swapaxes(query_weight, 0, 1).reshape(slice_width * local_heads, QL)
     owner_row = (owner_place[:, None] * step_count + step_index[None, :]).reshape(row_count)
     row_index = jnp.arange(row_count, dtype=jnp.int32)
-    same = request_row[None, :] == row_index[:, None]
-    slot_of_place = jnp.sum(jnp.where(same, owner_row[:, None], 0), axis=0)
 
     lane_rows = local_rows // NY
     width = slice_width * local_heads
     payload, own_fresh = project(
-        slot_of_place,
+        owner_place,
         jnp.stack([d * local_rows, y, c]),
         rows,
         other_rows,
@@ -425,17 +420,13 @@
     )
     head_values = head_values.astype(jnp.bfloat16).reshape(local_rows, local_heads * value_width)
     head_values = share(head_values, "z", NZ).reshape(NZ * local_rows, -1)
-    head_values = jnp.concatenate(
-        [head_values]
-        + [
-            lax.ppermute(head_values, "x", [(i, (i + k) % NX) for i in range(NX)])
-            for k in range(1, NX)
-        ]
-    )
+    head_values = jnp.concatenate(ring(head_values, "x"))
 
     turned = row_index.reshape(dp_count, NY, lane_rows).swapaxes(0, 1).reshape(row_count)
     turned_owner = owner_row.reshape(dp_count, NY, lane_rows).swapaxes(0, 1).reshape(row_count)
-    held = (x - row_index // (NZ * local_rows)) % NX * (NZ * local_rows)
+    relative = row_index // (NZ * local_rows)
+    relative = jnp.where(relative == 1, 3, jnp.where(relative == 0, 0, relative - 1))
+    held = (x + relative) % NX * (NZ * local_rows)
     held = held + row_index % (NZ * local_rows)
     turn = (turned_owner[:, None] == held[None, :]).astype(jnp.bfloat16)
     head_values = jnp.dot(turn, head_values, preferred_element_type=jnp.float32)
@@ -462,10 +453,10 @@
     residual = residual.reshape(NZ * HALF, -1)
     halves = jnp.concatenate([residual[: NZ // 2 * HALF], parts]), residual[NZ // 2 * HALF :]
 
-    def whole(parts):
-        return jnp.stack(parts[:3] + (jnp.concatenate(parts[3:]),))
-
-    pieces = ring(whole(ring(halves[0], "x")), "y") + ring(whole(ring(halves[1], "y")), "x")
+    def whole(block, axis):
+        return jnp.stack([block] + [shift(block, axis, step) for step in (1, -1, 2)])
+
+    pieces = ring(whole(halves[0], "x"), "y") + ring(whole(halves[1], "y"), "x")
     place_of = jnp.stack([x, y, c])
     vocab_width = head_weight.shape[1]
     head_weight = head_weight.reshape(NX, NZ, NC, HALF, vocab_width)

time: 267 us -> 263 us (0.985)
  blocking collectives: 69.4 us -> 46.4 us
  starting transfers between devices: 51.3 us -> 59.4 us
  waiting for transfers between devices: 80.7 us -> 88.1 us
  local copies, waits for them, and re-layouts: 19.1 us -> 22.8 us
    all_to_all x3 -> x2, blocking collectives: 59.7 us -> 36.5 us  [share(): return lax.all_to_all(copies, axes, split_axis=0, concat_axis=0, tiled=True)]
    ppermute x3 -> x0, waiting for transfers between devices: 20.9 us -> none  [on_device(): lax.ppermute(head_values, 'x', [(i, (i + k) % NX) for i in range(NX)])]
    all_to_all x3 -> x4, waiting for transfers between devices: 20.6 us -> 36.3 us  [share(): return lax.all_to_all(copies, axes, split_axis=0, concat_axis=0, tiled=True)]
    ppermute x16 -> x18, waiting for transfers between devices: 13.3 us -> 22.8 us  [shift(): return lax.ppermute(block, axis, [(i, (i + step) % 4) for i in range(4)])]
    all_to_all x3 -> x4, starting transfers between devices: 14.9 us -> 21.8 us  [share(): return lax.all_to_all(copies, axes, split_axis=0, concat_axis=0, tiled=True)]
    ppermute x16 -> x18, starting transfers between devices: 22.3 us -> 28.6 us  [shift(): return lax.ppermute(block, axis, [(i, (i + step) % 4) for i in range(4)])]
    ppermute x3 -> x0, starting transfers between devices: 5.08 us -> none  [on_device(): lax.ppermute(head_values, 'x', [(i, (i + k) % NX) for i in range(NX)])]
    unnamed x42 -> x46, local copies, waits for them, and re-layouts: 4.39 us -> 7.66 us
  transfers between devices with their start and end apart: 30 -> 30, of which waited for: 17 -> 20; matrix products, arithmetic and copies ran while one was open for 5% -> 5% of each run, Pallas kernels for 0% -> 0%
where the time goes in v3:
time: 263 us; the launch traced here: 262 us
  waiting for transfers between devices  88.1 us (33%)
  starting transfers between devices  59.4 us (23%)
  blocking collectives  46.4 us (18%)
  Pallas kernels  29.3 us (11%)
  local copies, waits for them, and re-layouts  22.8 us (9%)
  matrix products  7.38 us (3%)
  other arithmetic  7.05 us (3%)
    all_to_all x2, blocking collectives, share(): return lax.all_to_all(copies, axes, split_axis=0, concat_axis=0, tiled=True)  36.5 us
    all_to_all x4, waiting for transfers between devices, share(): return lax.all_to_all(copies, axes, split_axis=0, concat_axis=0, tiled=True)  36.3 us
    ppermute x18, starting transfers between devices, shift(): return lax.ppermute(block, axis, [(i, (i + step) % 4) for i in range(4)])  28.6 us
    ppermute x18, waiting for transfers between devices, shift(): return lax.ppermute(block, axis, [(i, (i + step) % 4) for i in range(4)])  22.8 us
    all_to_all x4, starting transfers between devices, share(): return lax.all_to_all(copies, axes, split_axis=0, concat_axis=0, tiled=True)  21.8 us
    pallas_call x1, Pallas kernels, attend(): pl.pallas_call(attend_kernel, out_shape=jax.ShapeDtypeStruct((slots, rows...  18.6 us
    all_to_all x1, waiting for transfers between devices, on_device(): lax.all_to_all(payload.reshape(dp_count, local_rows, -1), DP, split_axis=...  15.5 us
    all_to_all x1, blocking collectives, on_device(): lax.all_to_all(column_part.reshape(tp_count, own_rows, -1), TP, split_axi...  9.8 us
  transfers between devices with their start and end apart: 30, of which 20 were waited for; matrix products, arithmetic and copies ran while one was open for 5% of the time, Pallas kernels for 0%

profile of v3, /device:TPU:32, one launch (start us, length us, event | category | flops | bytes accessed | tf_op | source)
XLA Modules:
  0.0 261.7 jit_solution(8150427144383744928)
XLA Ops:
  1.9 3.4 %convolution_multiply_fusion = f32[16,264]{1,0:T(8,128)S(1)} fusion(bf16[7168,264]{0,1:T(8,128)(2,1)} %param.17, bf16[7168,16]{0,1:T(8,128)(2,1)} %param.15, f32[7168]{0:T(1024)} %param.16, f32[16]{0:T(128)S(1)} %add_rsqrt_fusion.2), kind=kOutput, calls=%fused_computation.6 | convolution fusion | flops 60903552 | bytes 4059712 | tf_op jit(solution)/shard_map/dot_general | solution.py:375
  5.4 9.8 %all_to_all.45 = f32[8,2,264]{2,1,0:T(2,128)S(1)} all-to-all(f32[8,2,264]{2,1,0:T(2,128)S(1)} %reshape.296), channel_id=1, replica_groups=mesh['x'=4,'z'=8,'y'=4,'c'=2] {'y','c'}, dimensions={0} | all-to-all | bytes 33792 | tf_op jit(solution)/shard_map/all_to_all | solution.py:380
  15.9 15.3 %all_to_all.46 = bf16[8,2,2176]{2,1,0:T(2,128)(2,1)S(1)} all-to-all(bf16[8,2,2176]{2,1,0:T(2,128)(2,1)S(1)} %broadcast_in_dim.47), channel_id=1, replica_groups=mesh['x'=4,'z'=8,'y'=4,'c'=2] {'z'}, dimensions={0} | all-to-all | bytes 139264 | tf_op jit(solution)/shard_map/all_to_all | solution.py:33
  31.3 21.2 %all_to_all.47 = bf16[16,16,2176]{2,1,0:T(8,128)(2,1)S(1)} all-to-all(bf16[16,16,2176]{2,1,0:T(8,128)(2,1)S(1)} %broadcast_in_dim.52), channel_id=1, replica_groups=mesh['x'=4,'z'=8,'y'=4,'c'=2] {'x','y'}, dimensions={0} | all-to-all | bytes 2228224 | tf_op jit(solution)/shard_map/all_to_all | solution.py:33
  52.6 2.8 %collective-permute-done.1.other_ref = bf16[256,2176]{1,0:T(8,128)(2,1)} collective-permute-done((bf16[256,2176]{1,0:T(8,128)(2,1)S(1)}, bf16[256,2176]{1,0:T(8,128)(2,1)}, u32[]{:S(2)}, u32[]{:S(2)}) %collective-permute-start.1) | collective-permute-done | bytes 1114144 | tf_op jit(solution)/shard_map/ppermute | solution.py:37
  56.6 2.7 %project.1 = (bf16[512,316]{1,0:T(8,128)(2,1)S(1)}, bf16[16,576]{1,0:T(8,128)(2,1)S(1)}) custom-call(s32[1,256]{1,0:T(1,128)S(1)} %bitcast.159, s32[3]{0:T(128)S(1)} %add_add_fusion.1.mine_ref, bf16[256,2176]{1,0:T(8,128)(2,1)S(1)} %bitcast.154, bf16[256,2176]{1,0:T(8,128)(2,1)} %collective-permute-done.1.other_ref, bf16[288,1536]{1,0:T(8,128)(2,1)S(1)} %bitcast.157, ...), custom_call_target="tpu_custom_call" | custom-call | tf_op jit(solution)/shard_map/project/pallas_call | solution.py:325
  60.1 5.1 %all-to-all-start.3 = ((bf16[32,16,316]{2,1,0:T(8,128)(2,1)}), bf16[32,16,316]{2,1,0:T(8,128)(2,1)S(1)}, u32[]{:S(2)}, u32[]{:S(2)}) async-start(bf16[32,16,316]{2,1,0:T(8,128)(2,1)} %bitcast.158), calls=%async_computation.3 | async-start | bytes 786432 | tf_op jit(solution)/shard_map/all_to_all | solution.py:408
  65.3 15.5 %all-to-all-done.3 = bf16[32,16,316]{2,1,0:T(8,128)(2,1)S(1)} async-done(((bf16[32,16,316]{2,1,0:T(8,128)(2,1)}), bf16[32,16,316]{2,1,0:T(8,128)(2,1)S(1)}, u32[]{:S(2)}, u32[]{:S(2)}) %all-to-all-start.3) | async-done | bytes 323616 | tf_op jit(solution)/shard_map/all_to_all | solution.py:408
  83.2 18.6 %attend.1 = bf16[8,32,512]{2,1,0:T(8,128)(2,1)S(1)} custom-call(s32[8]{0:T(128)S(1)} %copy-done.6, bf16[16,288,32]{2,1,0:T(8,128)(2,1)S(1)} %bitcast.152, bf16[8,16,576]{2,1,0:T(8,128)(2,1)S(1)} %pad.9.fresh_ref, bf16[8,576,4096]{2,1,0:T(8,128)(2,1)} %bitcast.160), custom_call_target="tpu_custom_call" | custom-call | tf_op jit(solution)/shard_map/attend/pallas_call | solution.py:146
  103.2 4.8 %all-to-all-start.4 = ((bf16[8,16,2048]{2,1,0:T(8,128)(2,1)}), bf16[8,16,2048]{2,1,0:T(8,128)(2,1)S(1)}, u32[]{:S(2)}, u32[]{:S(2)}) async-start(bf16[8,16,2048]{2,1,0:T(8,128)(2,1)} %broadcast_in_dim.54), calls=%async_computation.4 | async-start | bytes 1048576 | tf_op jit(solution)/shard_map/all_to_all | solution.py:33
  108.4 15.7 %all-to-all-done.4 = bf16[8,16,2048]{2,1,0:T(8,128)(2,1)S(1)} async-done(((bf16[8,16,2048]{2,1,0:T(8,128)(2,1)}), bf16[8,16,2048]{2,1,0:T(8,128)(2,1)S(1)}, u32[]{:S(2)}, u32[]{:S(2)}) %all-to-all-start.4) | async-done | bytes 524320 | tf_op jit(solution)/shard_map/all_to_all | solution.py:33
  124.1 4.3 %collective-permute-start.3 = (bf16[128,2048]{1,0:T(8,128)(2,1)S(1)}, bf16[128,2048]{1,0:T(8,128)(2,1)S(1)}, u32[]{:S(2)}, u32[]{:S(2)}) collective-permute-start(bf16[128,2048]{1,0:T(8,128)(2,1)S(1)} %bitcast.165), channel_id=1, source_target_pairs={{0,192},{64,0},{128,64},{192,128},{1,193},{65,1},{129,65},{193,129... | collective-permute-start | bytes 1572872 | tf_op jit(solution)/shard_map/ppermute | solution.py:41
  129.6 7.4 %collective-permute-done.2 = bf16[128,2048]{1,0:T(8,128)(2,1)S(1)} collective-permute-done((bf16[128,2048]{1,0:T(8,128)(2,1)S(1)}, bf16[128,2048]{1,0:T(8,128)(2,1)S(1)}, u32[]{:S(2)}, u32[]{:S(2)}) %collective-permute-start.2) | collective-permute-done | bytes 524320 | tf_op jit(solution)/shard_map/ppermute | solution.py:41
  137.3 3.3 %collective-permute-start.5 = (bf16[64,2048]{1,0:T(8,128)(2,1)S(1)}, bf16[64,2048]{1,0:T(8,128)(2,1)S(1)}, u32[]{:S(2)}, u32[]{:S(2)}) collective-permute-start(bf16[64,2048]{1,0:T(8,128)(2,1)S(1)} %slice.110), channel_id=1, source_target_pairs={{0,192},{64,0},{128,64},{192,128},{1,193},{65,1},{129,65},{193,129... | collective-permute-start | bytes 786440 | tf_op jit(solution)/shard_map/ppermute | solution.py:41
  142.3 2.5 collective-permute-done.4
  146.3 3.5 %fusion.8 = f32[512,224]{0,1:T(8,128)S(1)} fusion(bf16[224,2048]{1,0:T(8,128)(2,1)S(1)} %copy-done.19, bf16[512,2048]{1,0:T(8,128)(2,1)} %constant_dynamic-update-slice_fusion, s32[512]{0:T(512)S(1)} %fusion.41, s32[512]{0:T(512)S(1)} %eq.60), kind=kOutput, calls=%fused_computation.7 | convolution fusion | flops 1544814592 | bytes 3477504 | tf_op jit(solution)/shard_map/dot_general | solution.py:434
  152.2 3.4 %all-to-all-start.5 = ((f32[4,112,128]{2,1,0:T(8,128)}), f32[4,112,128]{2,1,0:T(8,128)S(1)}, u32[]{:S(2)}, u32[]{:S(2)}) async-start(f32[4,112,128]{2,1,0:T(8,128)} %copy.116), calls=%async_computation.5 | async-start | bytes 458752 | tf_op jit(solution)/shard_map/all_to_all | solution.py:442
  157.0 5.5 %all-to-all-done.5 = f32[4,112,128]{2,1,0:T(8,128)S(1)} async-done(((f32[4,112,128]{2,1,0:T(8,128)}), f32[4,112,128]{2,1,0:T(8,128)S(1)}, u32[]{:S(2)}, u32[]{:S(2)}) %all-to-all-start.5) | async-done | bytes 229408 | tf_op jit(solution)/shard_map/all_to_all | solution.py:442
  163.2 7.0 %all-to-all-start.6 = ((bf16[8,112,128]{2,1,0:T(8,128)(2,1)}), bf16[8,112,128]{2,1,0:T(8,128)(2,1)S(1)}, u32[]{:S(2)}, u32[]{:S(2)}) async-start(bf16[8,112,128]{2,1,0:T(8,128)(2,1)} %broadcast_in_dim.55), calls=%async_computation.6 | async-start | bytes 458752 | tf_op jit(solution)/shard_map/all_to_all | solution.py:33
  170.2 2.9 %dynamic-slice_bitcast_fusion = bf16[4,8,112,256]{3,2,1,0:T(8,128)(2,1)} fusion(bf16[4,8,2,112,256]{4,3,2,1,0:T(8,128)(2,1)} %bitcast.161, s32[]{:T(128)S(6)} %select_n.75), kind=kLoop, calls=%fused_computation.3 | loop fusion | bytes 3670020 | tf_op jit(solution)/shard_map/jit(dynamic_index_in_dim)/squeeze | solution.py:463
  173.1 6.3 %all-to-all-done.6 = bf16[8,112,128]{2,1,0:T(8,128)(2,1)S(1)} async-done(((bf16[8,112,128]{2,1,0:T(8,128)(2,1)}), bf16[8,112,128]{2,1,0:T(8,128)(2,1)S(1)}, u32[]{:S(2)}, u32[]{:S(2)}) %all-to-all-start.6) | async-done | bytes 229408 | tf_op jit(solution)/shard_map/all_to_all | solution.py:33
  191.5 2.7 %collective-permute-start.12 = (bf16[4,464,128]{2,1,0:T(8,128)(2,1)S(1)}, bf16[4,464,128]{2,1,0:T(8,128)(2,1)S(1)}, u32[]{:S(2)}, u32[]{:S(2)}) collective-permute-start(bf16[4,464,128]{2,1,0:T(8,128)(2,1)S(1)} %pad_maximum_fusion.rest_0_), channel_id=1, source_target_pairs={{0,6},{2,0},{4,2},{6,4},{1,7},{3,1},{5,3},{7,5},{8,14},{10,8},{12,... | collective-permute-start | bytes 1425416 | tf_op jit(solution)/shard_map/ppermute | solution.py:41
  194.2 2.6 collective-permute-done.17
  197.3 3.6 %collective-permute-start.19 = (bf16[4,448,128]{2,1,0:T(8,128)(2,1)S(1)}, bf16[4,448,128]{2,1,0:T(8,128)(2,1)S(1)}, u32[]{:S(2)}, u32[]{:S(2)}) collective-permute-start(bf16[4,448,128]{2,1,0:T(8,128)(2,1)S(1)} %pad_maximum_fusion.1.rest_5_), channel_id=1, source_target_pairs={{0,192},{64,0},{128,64},{192,128},{1,193},{65,1},{129,65},{193,129... | collective-permute-start | bytes 1376264 | tf_op jit(solution)/shard_map/ppermute | solution.py:41
  200.9 4.5 %collective-permute-done.11.rest_1_ = bf16[4,464,128]{2,1,0:T(8,128)(2,1)S(1)} collective-permute-done((bf16[4,464,128]{2,1,0:T(8,128)(2,1)S(1)}, bf16[4,464,128]{2,1,0:T(8,128)(2,1)S(1)}, u32[]{:S(2)}, u32[]{:S(2)}) %collective-permute-start.11) | collective-permute-done | bytes 475168 | tf_op jit(solution)/shard_map/ppermute | solution.py:41
  205.5 3.3 %collective-permute-start.14 = (bf16[2,464,128]{2,1,0:T(8,128)(2,1)S(1)}, bf16[2,464,128]{2,1,0:T(8,128)(2,1)}, u32[]{:S(2)}, u32[]{:S(2)}) collective-permute-start(bf16[2,464,128]{2,1,0:T(8,128)(2,1)S(1)} %slice.114), channel_id=1, source_target_pairs={{0,6},{2,0},{4,2},{6,4},{1,7},{3,1},{5,3},{7,5},{8,14},{10,8},{12,... | collective-permute-start | bytes 712712 | tf_op jit(solution)/shard_map/ppermute | solution.py:41
  211.2 2.4 collective-permute-start.21
  217.6 8.0 %head.1 = f32[2,4,128,256]{3,2,1,0:T(8,128)} custom-call(s32[3]{0:T(128)} %add_add_fusion.place_ref, f32[4,2,8,112]{3,2,1,0:T(8,128)} %bitcast.180, bf16[4,8,2,112,256]{4,3,2,1,0:T(8,128)(2,1)} %bitcast.162, bf16[4,8,112,256]{3,2,1,0:T(8,128)(2,1)} %collective-permute-done.other_hbm, bf16[4,464,128]{2,1,0:T(8,128)(2,1)} %copy-done.8, ...), custom_call_target="tpu_custom_call" | custom-call | tf_op jit(solution)/shard_map/head/pallas_call | solution.py:253
  232.2 3.3 %all-to-all-start.7 = ((f32[4,3,4,128]{3,2,1,0:T(4,128)}), f32[4,3,4,128]{3,2,1,0:T(4,128)S(1)}, u32[]{:S(2)}, u32[]{:S(2)}) async-start(f32[4,3,4,128]{3,2,1,0:T(4,128)} %broadcast_in_dim.56), calls=%async_computation.7 | async-start | bytes 49152 | tf_op jit(solution)/shard_map/all_to_all | solution.py:33
  236.0 4.9 %all-to-all-done.7 = f32[4,3,4,128]{3,2,1,0:T(4,128)S(1)} async-done(((f32[4,3,4,128]{3,2,1,0:T(4,128)}), f32[4,3,4,128]{3,2,1,0:T(4,128)S(1)}, u32[]{:S(2)}, u32[]{:S(2)}) %all-to-all-start.7) | async-done | bytes 24608 | tf_op jit(solution)/shard_map/all_to_all | solution.py:33
  241.6 6.7 %all-to-all-start.8 = ((f32[32,3,4,128]{3,2,1,0:T(4,128)}), f32[32,3,4,128]{3,2,1,0:T(4,128)S(1)}, u32[]{:S(2)}, u32[]{:S(2)}) async-start(f32[32,3,4,128]{3,2,1,0:T(4,128)} %broadcast_in_dim.60), calls=%async_computation.8 | async-start | bytes 393216 | tf_op jit(solution)/shard_map/all_to_all | solution.py:33
  249.3 9.4 %all-to-all-done.8 = f32[32,3,4,128]{3,2,1,0:T(4,128)S(1)} async-done(((f32[32,3,4,128]{3,2,1,0:T(4,128)}), f32[32,3,4,128]{3,2,1,0:T(4,128)S(1)}, u32[]{:S(2)}, u32[]{:S(2)}) %all-to-all-start.8) | async-done | bytes 196640 | tf_op jit(solution)/shard_map/all_to_all | solution.py:33
  (187 shorter events, 48.1 us)
Async XLA Ops:
  0.6 101.2 %copy-start = (bf16[16,512,128]{2,1,0:T(8,128)(2,1)S(1)}, bf16[16,512,128]{2,1,0:T(8,128)(2,1)}, u32[]{:S(2)}) copy-start(bf16[16,512,128]{2,1,0:T(8,128)(2,1)} %param.25) | copy-start | bytes 6291460
  5.3 50.1 %copy-start.5 = (s32[256]{0:T(256)S(1)}, s32[256]{0:T(256)}, u32[]{:S(2)}) copy-start(s32[256]{0:T(256)} %param.23) | copy-start | bytes 3076
  52.5 2.9 %collective-permute-start.1 = (bf16[256,2176]{1,0:T(8,128)(2,1)S(1)}, bf16[256,2176]{1,0:T(8,128)(2,1)}, u32[]{:S(2)}, u32[]{:S(2)}) collective-permute-start(bf16[256,2176]{1,0:T(8,128)(2,1)S(1)} %bitcast.153), channel_id=1, source_target_pairs={{0,1},{1,0},{2,3},{3,2},{4,5},{5,4},{6,7},{7,6},{8,9},{9,8},{10,11... | collective-permute-start | bytes 3342344 | tf_op jit(solution)/shard_map/ppermute | solution.py:37
  60.1 20.7 %all-to-all-start.3 = ((bf16[32,16,316]{2,1,0:T(8,128)(2,1)}), bf16[32,16,316]{2,1,0:T(8,128)(2,1)S(1)}, u32[]{:S(2)}, u32[]{:S(2)}) async-start(bf16[32,16,316]{2,1,0:T(8,128)(2,1)} %bitcast.158), calls=%async_computation.3 | async-start | bytes 786432 | tf_op jit(solution)/shard_map/all_to_all | solution.py:408
  103.2 20.9 %all-to-all-start.4 = ((bf16[8,16,2048]{2,1,0:T(8,128)(2,1)}), bf16[8,16,2048]{2,1,0:T(8,128)(2,1)S(1)}, u32[]{:S(2)}, u32[]{:S(2)}) async-start(bf16[8,16,2048]{2,1,0:T(8,128)(2,1)} %broadcast_in_dim.54), calls=%async_computation.4 | async-start | bytes 1048576 | tf_op jit(solution)/shard_map/all_to_all | solution.py:33
  124.1 12.9 %collective-permute-start.2 = (bf16[128,2048]{1,0:T(8,128)(2,1)S(1)}, bf16[128,2048]{1,0:T(8,128)(2,1)S(1)}, u32[]{:S(2)}, u32[]{:S(2)}) collective-permute-start(bf16[128,2048]{1,0:T(8,128)(2,1)S(1)} %bitcast.164), channel_id=1, source_target_pairs={{0,64},{64,128},{128,192},{192,0},{1,65},{65,129},{129,193},{193,1... | collective-permute-start | bytes 1572872 | tf_op jit(solution)/shard_map/ppermute | solution.py:41
  124.1 13.2 %collective-permute-start.3 = (bf16[128,2048]{1,0:T(8,128)(2,1)S(1)}, bf16[128,2048]{1,0:T(8,128)(2,1)S(1)}, u32[]{:S(2)}, u32[]{:S(2)}) collective-permute-start(bf16[128,2048]{1,0:T(8,128)(2,1)S(1)} %bitcast.165), channel_id=1, source_target_pairs={{0,192},{64,0},{128,64},{192,128},{1,193},{65,1},{129,65},{193,129... | collective-permute-start | bytes 1572872 | tf_op jit(solution)/shard_map/ppermute | solution.py:41
  137.0 7.8 %collective-permute-start.4 = (bf16[64,2048]{1,0:T(8,128)(2,1)S(1)}, bf16[64,2048]{1,0:T(8,128)(2,1)S(1)}, u32[]{:S(2)}, u32[]{:S(2)}) collective-permute-start(bf16[64,2048]{1,0:T(8,128)(2,1)S(1)} %slice.109), channel_id=1, source_target_pairs={{0,64},{64,128},{128,192},{192,0},{1,65},{65,129},{129,193},{193,1... | collective-permute-start | bytes 786440 | tf_op jit(solution)/shard_map/ppermute | solution.py:41
  137.3 8.2 %collective-permute-start.5 = (bf16[64,2048]{1,0:T(8,128)(2,1)S(1)}, bf16[64,2048]{1,0:T(8,128)(2,1)S(1)}, u32[]{:S(2)}, u32[]{:S(2)}) collective-permute-start(bf16[64,2048]{1,0:T(8,128)(2,1)S(1)} %slice.110), channel_id=1, source_target_pairs={{0,192},{64,0},{128,64},{192,128},{1,193},{65,1},{129,65},{193,129... | collective-permute-start | bytes 786440 | tf_op jit(solution)/shard_map/ppermute | solution.py:41
  149.8 1.6 collective-permute-start.6
  152.2 10.3 %all-to-all-start.5 = ((f32[4,112,128]{2,1,0:T(8,128)}), f32[4,112,128]{2,1,0:T(8,128)S(1)}, u32[]{:S(2)}, u32[]{:S(2)}) async-start(f32[4,112,128]{2,1,0:T(8,128)} %copy.116), calls=%async_computation.5 | async-start | bytes 458752 | tf_op jit(solution)/shard_map/all_to_all | solution.py:442
  163.2 16.1 %all-to-all-start.6 = ((bf16[8,112,128]{2,1,0:T(8,128)(2,1)}), bf16[8,112,128]{2,1,0:T(8,128)(2,1)S(1)}, u32[]{:S(2)}, u32[]{:S(2)}) async-start(bf16[8,112,128]{2,1,0:T(8,128)(2,1)} %broadcast_in_dim.55), calls=%async_computation.6 | async-start | bytes 458752 | tf_op jit(solution)/shard_map/all_to_all | solution.py:33
  173.1 41.9 %collective-permute-start = (bf16[4,8,112,256]{3,2,1,0:T(8,128)(2,1)}, bf16[4,8,112,256]{3,2,1,0:T(8,128)(2,1)}, u32[]{:S(2)}, u32[]{:S(2)}) collective-permute-start(bf16[4,8,112,256]{3,2,1,0:T(8,128)(2,1)} %dynamic-slice_bitcast_fusion), channel_id=1, source_target_pairs={{0,1},{1,0},{2,3},{3,2},{4,5},{5,4},{6,7},{7,6},{8,9},{9,8},{10,11... | collective-permute-start | bytes 5505032 | tf_op jit(solution)/shard_map/ppermute | solution.py:37
  179.5 1.2 collective-permute-start.7
  180.8 6.6 %collective-permute-start.8 = (bf16[464,128]{1,0:T(8,128)(2,1)S(1)}, bf16[464,128]{1,0:T(8,128)(2,1)S(1)}, u32[]{:S(2)}, u32[]{:S(2)}) collective-permute-start(bf16[464,128]{1,0:T(8,128)(2,1)S(1)} %get-tuple-element.16), channel_id=1, source_target_pairs={{0,64},{64,128},{128,192},{192,0},{1,65},{65,129},{129,193},{193,1... | collective-permute-start | bytes 356360 | tf_op jit(solution)/shard_map/ppermute | solution.py:41
  182.0 7.3 %collective-permute-start.9 = (bf16[464,128]{1,0:T(8,128)(2,1)S(1)}, bf16[464,128]{1,0:T(8,128)(2,1)S(1)}, u32[]{:S(2)}, u32[]{:S(2)}) collective-permute-start(bf16[464,128]{1,0:T(8,128)(2,1)S(1)} %get-tuple-element.16), channel_id=1, source_target_pairs={{0,192},{64,0},{128,64},{192,128},{1,193},{65,1},{129,65},{193,129... | collective-permute-start | bytes 356360 | tf_op jit(solution)/shard_map/ppermute | solution.py:41
  184.1 6.7 %collective-permute-start.10 = (bf16[464,128]{1,0:T(8,128)(2,1)S(1)}, bf16[464,128]{1,0:T(8,128)(2,1)S(1)}, u32[]{:S(2)}, u32[]{:S(2)}) collective-permute-start(bf16[464,128]{1,0:T(8,128)(2,1)S(1)} %get-tuple-element.16), channel_id=1, source_target_pairs={{0,128},{64,192},{128,0},{192,64},{1,129},{65,193},{129,1},{193,65... | collective-permute-start | bytes 356360 | tf_op jit(solution)/shard_map/ppermute | solution.py:41
  185.0 6.5 %collective-permute-start.15 = (bf16[448,128]{1,0:T(8,128)(2,1)S(1)}, bf16[448,128]{1,0:T(8,128)(2,1)S(1)}, u32[]{:S(2)}, u32[]{:S(2)}) collective-permute-start(bf16[448,128]{1,0:T(8,128)(2,1)S(1)} %bitcast.170), channel_id=1, source_target_pairs={{0,2},{2,4},{4,6},{6,0},{1,3},{3,5},{5,7},{7,1},{8,10},{10,12},{12... | collective-permute-start | bytes 344072 | tf_op jit(solution)/shard_map/ppermute | solution.py:41
  187.4 6.8 %collective-permute-start.16 = (bf16[448,128]{1,0:T(8,128)(2,1)S(1)}, bf16[448,128]{1,0:T(8,128)(2,1)S(1)}, u32[]{:S(2)}, u32[]{:S(2)}) collective-permute-start(bf16[448,128]{1,0:T(8,128)(2,1)S(1)} %bitcast.171), channel_id=1, source_target_pairs={{0,6},{2,0},{4,2},{6,4},{1,7},{3,1},{5,3},{7,5},{8,14},{10,8},{12,... | collective-permute-start | bytes 344072 | tf_op jit(solution)/shard_map/ppermute | solution.py:41
  189.2 7.5 %collective-permute-start.17 = (bf16[448,128]{1,0:T(8,128)(2,1)S(1)}, bf16[448,128]{1,0:T(8,128)(2,1)S(1)}, u32[]{:S(2)}, u32[]{:S(2)}) collective-permute-start(bf16[448,128]{1,0:T(8,128)(2,1)S(1)} %bitcast.172), channel_id=1, source_target_pairs={{0,4},{2,6},{4,0},{6,2},{1,5},{3,7},{5,1},{7,3},{8,12},{10,14},{12... | collective-permute-start | bytes 344072 | tf_op jit(solution)/shard_map/ppermute | solution.py:41
  190.9 14.5 %collective-permute-start.11 = (bf16[4,464,128]{2,1,0:T(8,128)(2,1)S(1)}, bf16[4,464,128]{2,1,0:T(8,128)(2,1)S(1)}, u32[]{:S(2)}, u32[]{:S(2)}) collective-permute-start(bf16[4,464,128]{2,1,0:T(8,128)(2,1)S(1)} %pad_maximum_fusion.rest_0_), channel_id=1, source_target_pairs={{0,2},{2,4},{4,6},{6,0},{1,3},{3,5},{5,7},{7,1},{8,10},{10,12},{12... | collective-permute-start | bytes 1425416 | tf_op jit(solution)/shard_map/ppermute | solution.py:41
  191.5 13.9 %collective-permute-start.12 = (bf16[4,464,128]{2,1,0:T(8,128)(2,1)S(1)}, bf16[4,464,128]{2,1,0:T(8,128)(2,1)S(1)}, u32[]{:S(2)}, u32[]{:S(2)}) collective-permute-start(bf16[4,464,128]{2,1,0:T(8,128)(2,1)S(1)} %pad_maximum_fusion.rest_0_), channel_id=1, source_target_pairs={{0,6},{2,0},{4,2},{6,4},{1,7},{3,1},{5,3},{7,5},{8,14},{10,8},{12,... | collective-permute-start | bytes 1425416 | tf_op jit(solution)/shard_map/ppermute | solution.py:41
  196.8 11.9 %collective-permute-start.18 = (bf16[4,448,128]{2,1,0:T(8,128)(2,1)S(1)}, bf16[4,448,128]{2,1,0:T(8,128)(2,1)S(1)}, u32[]{:S(2)}, u32[]{:S(2)}) collective-permute-start(bf16[4,448,128]{2,1,0:T(8,128)(2,1)S(1)} %pad_maximum_fusion.1.rest_5_), channel_id=1, source_target_pairs={{0,64},{64,128},{128,192},{192,0},{1,65},{65,129},{129,193},{193,1... | collective-permute-start | bytes 1376264 | tf_op jit(solution)/shard_map/ppermute | solution.py:41
  197.3 13.1 %collective-permute-start.19 = (bf16[4,448,128]{2,1,0:T(8,128)(2,1)S(1)}, bf16[4,448,128]{2,1,0:T(8,128)(2,1)S(1)}, u32[]{:S(2)}, u32[]{:S(2)}) collective-permute-start(bf16[4,448,128]{2,1,0:T(8,128)(2,1)S(1)} %pad_maximum_fusion.1.rest_5_), channel_id=1, source_target_pairs={{0,192},{64,0},{128,64},{192,128},{1,193},{65,1},{129,65},{193,129... | collective-permute-start | bytes 1376264 | tf_op jit(solution)/shard_map/ppermute | solution.py:41
  205.4 12.2 %collective-permute-start.13 = (bf16[2,464,128]{2,1,0:T(8,128)(2,1)S(1)}, bf16[2,464,128]{2,1,0:T(8,128)(2,1)}, u32[]{:S(2)}, u32[]{:S(2)}) collective-permute-start(bf16[2,464,128]{2,1,0:T(8,128)(2,1)S(1)} %slice.113), channel_id=1, source_target_pairs={{0,2},{2,4},{4,6},{6,0},{1,3},{3,5},{5,7},{7,1},{8,10},{10,12},{12... | collective-permute-start | bytes 712712 | tf_op jit(solution)/shard_map/ppermute | solution.py:41
  205.5 12.0 %collective-permute-start.14 = (bf16[2,464,128]{2,1,0:T(8,128)(2,1)S(1)}, bf16[2,464,128]{2,1,0:T(8,128)(2,1)}, u32[]{:S(2)}, u32[]{:S(2)}) collective-permute-start(bf16[2,464,128]{2,1,0:T(8,128)(2,1)S(1)} %slice.114), channel_id=1, source_target_pairs={{0,6},{2,0},{4,2},{6,4},{1,7},{3,1},{5,3},{7,5},{8,14},{10,8},{12,... | collective-permute-start | bytes 712712 | tf_op jit(solution)/shard_map/ppermute | solution.py:41
  209.6 7.5 %collective-permute-start.20 = (bf16[2,448,128]{2,1,0:T(8,128)(2,1)}, bf16[2,448,128]{2,1,0:T(8,128)(2,1)}, u32[]{:S(2)}, u32[]{:S(2)}) collective-permute-start(bf16[2,448,128]{2,1,0:T(8,128)(2,1)} %slice.116), channel_id=1, source_target_pairs={{0,64},{64,128},{128,192},{192,0},{1,65},{65,129},{129,193},{193,1... | collective-permute-start | bytes 688136 | tf_op jit(solution)/shard_map/ppermute | solution.py:41
  211.2 6.3 %collective-permute-start.21 = (bf16[2,448,128]{2,1,0:T(8,128)(2,1)}, bf16[2,448,128]{2,1,0:T(8,128)(2,1)}, u32[]{:S(2)}, u32[]{:S(2)}) collective-permute-start(bf16[2,448,128]{2,1,0:T(8,128)(2,1)} %slice.117), channel_id=1, source_target_pairs={{0,192},{64,0},{128,64},{192,128},{1,193},{65,1},{129,65},{193,129... | collective-permute-start | bytes 688136 | tf_op jit(solution)/shard_map/ppermute | solution.py:41
  226.7 2.0 collective-permute-start.22
  230.3 1.3 collective-permute-start.23
  232.2 8.6 %all-to-all-start.7 = ((f32[4,3,4,128]{3,2,1,0:T(4,128)}), f32[4,3,4,128]{3,2,1,0:T(4,128)S(1)}, u32[]{:S(2)}, u32[]{:S(2)}) async-start(f32[4,3,4,128]{3,2,1,0:T(4,128)} %broadcast_in_dim.56), calls=%async_computation.7 | async-start | bytes 49152 | tf_op jit(solution)/shard_map/all_to_all | solution.py:33
  241.6 17.1 %all-to-all-start.8 = ((f32[32,3,4,128]{3,2,1,0:T(4,128)}), f32[32,3,4,128]{3,2,1,0:T(4,128)S(1)}, u32[]{:S(2)}, u32[]{:S(2)}) async-start(f32[32,3,4,128]{3,2,1,0:T(4,128)} %broadcast_in_dim.60), calls=%async_computation.8 | async-start | bytes 393216 | tf_op jit(solution)/shard_map/all_to_all | solution.py:33
  (18 other events, 273.2 us)
